TPU v7x, 32 devices: a whole 2x2x4 slice. The times are simulated.
32 devices in a mesh: dp: 4 (over y, x), tensor: 8 (over z, core).
Axes of the slice: x: 2, y: 2, z: 4, core: 2. Of those that a mesh axis runs over, the one named last changes fastest.
Arguments:
- grad_out: bfloat16 [4096, 8192], P(('dp', 'tensor')), may hold values from -6 to 6
- out_weight: bfloat16 [8192, 4096], P('dp', 'tensor'), may hold values from -0.0625 to 0.0625
- query: bfloat16 [4096, 4096], P('dp', 'tensor'), may hold values from -6 to 6, as said below
- keys: bfloat16 [4096, 256], P('dp'), may hold values from -6 to 6
- values: bfloat16 [4096, 256], P('dp'), may hold values from -6 to 6
- attended: bfloat16 [4096, 4096], P('dp', 'tensor'), may hold values from -6 to 6, as said below
- stats: float32 [32, 4096], P('tensor', 'dp'), as said below
Outputs:
- query_grad: bfloat16 [4096, 4096], P('dp', 'tensor')
- key_grad: bfloat16 [4096, 256], P('dp', 'tensor')
- value_grad: bfloat16 [4096, 256], P('dp', 'tensor')
- weight_grad: bfloat16 [8192, 4096], P('dp', 'tensor')
Inputs may be any that keep to these rules, and one draw needn't show every extreme that they name: query, keys and values are independent draws. attended is the causal attention output of the given query, keys and values within each sequence of 1024 rows: query head h uses key head h // 16, scores scaled by 128 ** -0.5, softmax over keys at or before the query. stats[h, t] is the logarithm of the sum of exp(score) over the keys that row t of head h attends to, for the same scores.
All inputs are finite; a program needn't handle non-finite values.
Results may differ from a plain program's by a relative error of at most 0.013.
Values may be sent and summed in bfloat16 or wider, within the bound.
A program may use at most 192 MiB of HBM per device.

v0:
```python
import functools

import jax
import jax.numpy as jnp
from jax import lax
from jax.experimental import pallas as pl
from jax.experimental.pallas import tpu as pltpu
from jax.sharding import PartitionSpec as P


HD = 128
GROUP = 16
CHUNKS = 4


def partner(value, axis, mask):
    pairs = [(source, source ^ mask) for source in range(lax.axis_size(axis))]
    return lax.ppermute(value, axis, pairs)


def nt_dot(a, b):
    return lax.dot_general(a, b, (((1,), (1,)), ((), ())), preferred_element_type=jnp.float32)


def attention_kernel(block, q_ref, k_ref, kt_ref, v_ref, o_ref, g_ref, s_ref, dq_ref, dk_ref, dv_ref):
    head = pl.program_id(0)
    length = q_ref.shape[0]
    scale = HD ** (-0.5)

    @pl.when(head == 0)
    def _():
        dk_ref[...] = jnp.zeros_like(dk_ref)
        dv_ref[...] = jnp.zeros_like(dv_ref)

    ones = jnp.ones((8, HD), jnp.float32)
    for j in range(length // block):
        rows = pl.ds(j * block, block)
        span = (j + 1) * block
        q = q_ref[rows, :]
        g = g_ref[rows, :]
        product = g.astype(jnp.float32) * o_ref[rows, :].astype(jnp.float32)
        offset = lax.dot_general(
            ones, product, (((1,), (1,)), ((), ())),
            preferred_element_type=jnp.float32, precision=lax.Precision.HIGHEST,
        )[:1, :]
        stat = s_ref[pl.ds(head, 1), rows]
        scores = nt_dot(k_ref[:span, :], q) * scale
        key_pos = lax.broadcasted_iota(jnp.int32, (span, block), 0)
        query_pos = lax.broadcasted_iota(jnp.int32, (span, block), 1) + j * block
        attention = jnp.where(key_pos <= query_pos, jnp.exp(scores - stat), 0.0)
        grad_attention = nt_dot(v_ref[:span, :], g)
        grad_scores = (attention * (grad_attention - offset)).astype(jnp.bfloat16)
        dv_ref[:span, :] += jnp.dot(
            attention.astype(jnp.bfloat16), g, preferred_element_type=jnp.float32
        )
        dk_ref[:span, :] += jnp.dot(grad_scores, q, preferred_element_type=jnp.float32)
        dq_t = jnp.dot(kt_ref[:, :span], grad_scores, preferred_element_type=jnp.float32)
        dq_ref[rows, :] = (dq_t * scale).T.astype(dq_ref.dtype)

    @pl.when(head == pl.num_programs(0) - 1)
    def _():
        dk_ref[...] = dk_ref[...] * scale


def attention_grads(query, key_one, value_one, attended, grad_att, stats):
    length, width = query.shape
    heads = width // HD
    per_head = pl.BlockSpec((length, HD), lambda h: (0, h))
    shared = pl.BlockSpec((length, HD), lambda h: (0, 0))
    return pl.pallas_call(
        functools.partial(attention_kernel, 256),
        grid=(heads,),
        in_specs=[
            per_head,
            shared,
            pl.BlockSpec((HD, length), lambda h: (0, 0)),
            shared,
            per_head,
            per_head,
            pl.BlockSpec((heads, length), lambda h: (0, 0)),
        ],
        out_specs=[per_head, shared, shared],
        out_shape=[
            jax.ShapeDtypeStruct((length, width), jnp.bfloat16),
            jax.ShapeDtypeStruct((length, HD), jnp.float32),
            jax.ShapeDtypeStruct((length, HD), jnp.float32),
        ],
        compiler_params=pltpu.CompilerParams(
            dimension_semantics=("arbitrary",), vmem_limit_bytes=40 * 2**20
        ),
        cost_estimate=pl.CostEstimate(
            flops=10 * heads * length * length * HD,
            bytes_accessed=10 * length * width,
            transcendentals=heads * length * length,
        ),
        name="attention_grads",
    )(query, key_one, key_one.T, value_one, attended, grad_att, stats)


def add_term(total, chunk, part, weights):
    own, w_x, w_y, w_lo, w_hi = weights
    half_rows = w_lo.shape[0]
    if part.stop <= half_rows:
        far = w_lo[part]
    else:
        far = w_hi[part.start - half_rows : part.stop - half_rows]
    weight = jnp.concatenate([own[part], w_x[part], w_y[part], far], axis=0)
    term = jnp.dot(chunk, weight, preferred_element_type=jnp.float32)
    return term if total is None else total + term


def projection_chunked(grad_out, out_weight, attended):
    dp, tensor = lax.axis_size("dp"), lax.axis_size("tensor")
    me = lax.axis_index("dp")
    place = lax.axis_index("tensor")
    chips = tensor // 2
    ring = [(source, (source + 2) % tensor) for source in range(tensor)]
    local = grad_out.shape[0]
    rows, depth = out_weight.shape[0], out_weight.shape[0] // CHUNKS
    half_rows, half_depth = rows // 2, depth // 2
    w_x = partner(out_weight, "dp", 1)
    w_y = partner(out_weight, "dp", 2)
    order = []
    for k in range(chips):
        holder = (place + tensor - 2 * k) % tensor
        order += [holder, holder ^ 1]
    attended = jnp.concatenate(
        [lax.dynamic_slice_in_dim(attended, h * local, local, 0) for h in order], axis=0
    )
    total = None
    parts = []
    owned = []
    arrived = []
    for c in range(CHUNKS):
        mine = jnp.concatenate(
            [
                lax.dynamic_slice_in_dim(grad_out, (me ^ r) * rows + c * depth, depth, 1)
                for r in range(dp)
            ],
            axis=1,
        )
        if c >= 2:
            mine, arrived[c - 2][-2] = lax.optimization_barrier((mine, arrived[c - 2][-2]))
        slots = [mine]
        for _ in range(chips - 1):
            slots.append(lax.ppermute(slots[-1], "tensor", ring))
        arrived.append(slots)
    for c in range(CHUNKS):
        part = slice(c * depth, (c + 1) * depth)
        blocks = []
        for slot in arrived[c]:
            blocks += [slot, partner(slot, "tensor", 1)]
        if c == 0:
            blocks[0], w_x, w_y = lax.optimization_barrier((blocks[0], w_x, w_y))
        elif c == 1:
            w_lo = partner(w_y[:half_rows], "dp", 1)
            w_hi = partner(w_x[half_rows:], "dp", 2)
            blocks[0], w_lo, w_hi = lax.optimization_barrier((blocks[0], w_lo, w_hi))
        else:
            blocks[0], total, owned[-1] = lax.optimization_barrier((blocks[0], total, owned[-1]))
        chunk = jnp.concatenate(blocks, axis=0)
        partial = lax.dot_general(
            chunk, attended, (((0,), (0,)), ((), ())), preferred_element_type=jnp.float32
        ).astype(jnp.bfloat16)
        chunk, partial = lax.optimization_barrier((chunk, partial))
        partial = partial.reshape(dp, depth, -1)
        upper, lower = partial[:, :half_depth], partial[:, half_depth:]
        send_upper = jnp.stack([upper[1], upper[3]])
        send_lower = lower[2:4]
        parts.append((chunk, part))
        if c >= 1:
            for done, where in parts:
                total = add_term(total, done, where, (out_weight, w_x, w_y, w_lo, w_hi))
            parts = []
        if c == CHUNKS - 1:
            total, send_upper, send_lower = lax.optimization_barrier(
                (total, send_upper, send_lower)
            )
        got_upper = partner(send_upper, "dp", 1)
        got_lower = partner(send_lower, "dp", 2)
        keep = upper[0].astype(jnp.float32) + got_upper[0].astype(jnp.float32)
        pass_on = upper[2].astype(jnp.float32) + got_upper[1].astype(jnp.float32)
        out_upper = keep + partner(pass_on.astype(jnp.bfloat16), "dp", 2).astype(jnp.float32)
        keep = lower[0].astype(jnp.float32) + got_lower[0].astype(jnp.float32)
        pass_on = lower[1].astype(jnp.float32) + got_lower[1].astype(jnp.float32)
        out_lower = keep + partner(pass_on.astype(jnp.bfloat16), "dp", 1).astype(jnp.float32)
        owned.append(jnp.concatenate([out_upper, out_lower], axis=0).astype(jnp.bfloat16))
    grad_att = total.astype(jnp.bfloat16)
    unrolled = jnp.zeros_like(grad_att)
    for k, h in enumerate(order):
        unrolled = lax.dynamic_update_slice_in_dim(
            unrolled, grad_att[k * local : (k + 1) * local], h * local, 0
        )
    return unrolled, jnp.concatenate(owned, axis=0)


def projection_plain(grad_out, out_weight, attended):
    grad_rows = lax.all_gather(grad_out, "tensor", axis=0, tiled=True)
    grad_att = jnp.dot(
        grad_rows,
        lax.all_gather(out_weight, "dp", axis=0, tiled=True),
        preferred_element_type=jnp.float32,
    ).astype(jnp.bfloat16)
    weight_grad = lax.psum_scatter(
        lax.dot_general(
            grad_rows, attended, (((0,), (0,)), ((), ())), preferred_element_type=jnp.float32
        ).astype(jnp.bfloat16),
        "dp",
        scatter_dimension=0,
        tiled=True,
    )
    return grad_att, weight_grad


def per_device(grad_out, out_weight, query, keys, values, attended, stats):
    heads = query.shape[1] // HD
    project = projection_chunked if lax.axis_size("dp") == 4 else projection_plain
    grad_att, weight_grad = project(grad_out, out_weight, attended)
    tensor_index = lax.axis_index("tensor")
    key_head = tensor_index * heads // GROUP
    key_one = lax.dynamic_slice_in_dim(keys, key_head * HD, HD, 1)
    value_one = lax.dynamic_slice_in_dim(values, key_head * HD, HD, 1)
    query_grad, key_part, value_part = attention_grads(
        query, key_one, value_one, attended, grad_att, stats
    )
    group_span = GROUP // heads
    group_place = tensor_index % group_span
    bit_count = group_span.bit_length() - 1
    running_kv = jnp.stack([key_part, value_part])
    for bit_number in reversed(range(bit_count)):
        half_cols = running_kv.shape[2] // 2
        lower_cols = running_kv[:, :, :half_cols]
        upper_cols = running_kv[:, :, half_cols:]
        upper_half = group_place // (1 << bit_number) % 2 == 1
        kept_cols = jnp.where(upper_half, upper_cols, lower_cols)
        sent_cols = jnp.where(upper_half, lower_cols, upper_cols)
        running_kv = kept_cols + partner(
            sent_cols.astype(jnp.bfloat16), "tensor", 1 << bit_number
        ).astype(sent_cols.dtype)
    key_grad = running_kv[0].astype(jnp.bfloat16)
    value_grad = running_kv[1].astype(jnp.bfloat16)
    return (query_grad, key_grad, value_grad, weight_grad)


def solution(mesh):
    placed = (
        P(("dp", "tensor"), None),
        P("dp", "tensor"),
        P("dp", "tensor"),
        P("dp", None),
        P("dp", None),
        P("dp", "tensor"),
        P("tensor", "dp"),
    )
    return jax.shard_map(
        per_device,
        mesh=mesh,
        in_specs=placed,
        out_specs=(P("dp", "tensor"), P("dp", "tensor"), P("dp", "tensor"), P("dp", "tensor")),
        check_vma=False,
    )
```

profile of v0, /device:TPU:0, one launch (start us, length us, event | category | flops | bytes accessed | tf_op | source)
XLA Modules:
  0.0 277.5 jit_solution(13882125115735016048)
XLA Ops:
  0.6 3.0 %collective-permute-start.4 = (bf16[2048,512]{1,0:T(8,128)(2,1)}, bf16[2048,512]{1,0:T(8,128)(2,1)S(1)}, u32[]{:S(2)}, u32[]{:S(2)}) collective-permute-start(bf16[2048,512]{1,0:T(8,128)(2,1)} %param.8), channel_id=1, source_target_pairs={{0,8},{8,0},{16,24},{24,16},{1,9},{9,1},{17,25},{25,17},{2,10},{10... | collective-permute-start | bytes 6291464 | tf_op jit(solution)/shard_map/ppermute | solution.py:18
  3.7 1.5 collective-permute-start.5
  5.2 2.5 constant_dynamic-slice_fusion.3
  7.7 0.9 pad_maximum_fusion.4
  8.6 1.6 collective-permute-start.2
  10.2 0.8 pad_maximum_fusion.2
  11.0 1.6 collective-permute-start
  12.8 23.5 %collective-permute-done = bf16[128,2048]{1,0:T(8,128)(2,1)} collective-permute-done((bf16[128,2048]{1,0:T(8,128)(2,1)}, bf16[128,2048]{1,0:T(8,128)(2,1)}, u32[]{:S(2)}, u32[]{:S(2)}) %collective-permute-start) | collective-permute-done | bytes 524320 | tf_op jit(solution)/shard_map/ppermute | solution.py:146
  36.3 1.3 collective-permute-start.3
  37.6 1.3 pad_maximum_fusion.1
  38.9 1.2 fusion.67
  40.1 13.0 %collective-permute-done.1 = bf16[128,2048]{1,0:T(8,128)(2,1)S(1)} collective-permute-done((bf16[128,2048]{1,0:T(8,128)(2,1)}, bf16[128,2048]{1,0:T(8,128)(2,1)S(1)}, u32[]{:S(2)}, u32[]{:S(2)}) %collective-permute-start.1) | collective-permute-done | bytes 524320 | tf_op jit(solution)/shard_map/ppermute | solution.py:146
  53.1 10.0 %collective-permute-done.3 = bf16[128,2048]{1,0:T(8,128)(2,1)S(1)} collective-permute-done((bf16[128,2048]{1,0:T(8,128)(2,1)}, bf16[128,2048]{1,0:T(8,128)(2,1)S(1)}, u32[]{:S(2)}, u32[]{:S(2)}) %collective-permute-start.3) | collective-permute-done | bytes 524320 | tf_op jit(solution)/shard_map/ppermute | solution.py:146
  63.6 1.1 constant_dynamic-update-slice_fusion.7
  64.9 1.1 constant_dynamic-update-slice_fusion.6
  66.0 1.1 constant_dynamic-update-slice_fusion.5
  67.6 11.8 %collective-permute-done.9 = bf16[128,2048]{1,0:T(8,128)(2,1)S(1)} collective-permute-done((bf16[128,2048]{1,0:T(8,128)(2,1)S(1)}, bf16[128,2048]{1,0:T(8,128)(2,1)S(1)}, u32[]{:S(2)}, u32[]{:S(2)}) %collective-permute-start.9) | collective-permute-done | bytes 524320 | tf_op jit(solution)/shard_map/ppermute | solution.py:146
  79.4 1.3 slice.269
  82.3 2.4 convolution_convert_fusion.3
  84.9 3.6 %fusion.68 = (bf16[512,512]{1,0:T(8,128)(2,1)}, bf16[512,512]{1,0:T(8,128)(2,1)}, bf16[512,512]{1,0:T(8,128)(2,1)S(1)}, bf16[512,512]{1,0:T(8,128)(2,1)S(1)}, bf...) fusion(bf16[2048,512]{1,0:T(8,128)(2,1)S(1)} %collective-permut, ...), kind=kLoop, calls=%fused_computation.168 | loop fusion | bytes 8388608 | tf_op jit(solution)/shard_map/slice | solution.py:107
  88.5 18.0 %collective-permute-done.11 = bf16[1024,512]{1,0:T(8,128)(2,1)S(1)} collective-permute-done((bf16[1024,512]{1,0:T(8,128)(2,1)S(1)}, bf16[1024,512]{1,0:T(8,128)(2,1)S(1)}, u32[]{:S(2)}, u32[]{:S(2)}) %collective-permute-start.11) | collective-permute-done | bytes 1048608 | tf_op jit(solution)/shard_map/ppermute | solution.py:18
  106.9 1.1 constant_dynamic-update-slice_fusion.15
  108.1 1.1 constant_dynamic-update-slice_fusion.13
  109.5 24.8 %collective-permute-done.16 = bf16[128,2048]{1,0:T(8,128)(2,1)S(1)} collective-permute-done((bf16[128,2048]{1,0:T(8,128)(2,1)S(1)}, bf16[128,2048]{1,0:T(8,128)(2,1)S(1)}, u32[]{:S(2)}, u32[]{:S(2)}) %collective-permute-start.16) | collective-permute-done | bytes 524320 | tf_op jit(solution)/shard_map/ppermute | solution.py:146
  134.5 1.7 collective-permute-done.17
  136.2 2.4 convolution_convert_fusion.2
  140.1 1.1 fusion.72
  141.2 2.3 fusion.8
  143.5 9.3 %collective-permute-done.18 = bf16[2,256,512]{2,1,0:T(8,128)(2,1)S(1)} collective-permute-done((bf16[2,256,512]{2,1,0:T(8,128)(2,1)S(1)}, bf16[2,256,512]{2,1,0:T(8,128)(2,1)S(1)}, u32[]{:S(2)}, u32[]{:S(2)}) %collective-permute-start.18) | collective-permute-done | bytes 524320 | tf_op jit(solution)/shard_map/ppermute | solution.py:18
  154.0 1.3 collective-permute-start.21
  155.2 3.6 %fusion.38 = f32[1024,512]{1,0:T(8,128)} fusion(f32[1024,512]{1,0:T(8,128)S(1)} %fusion.8, bf16[1024,2048]{1,0:T(8,128)(2,1)S(1)} %constant_dynamic-update-slice_fusion, bf16[512,512]{1,0:T(8,128)(2,1)S(1)} %get-tuple-element.129, bf16[512,512]{1,0:T(8,128)(2,1)S(1)} %get-tuple-element.124, bf16[512,512]{1,0:T(8,128)(2,1)S(1)} %get-tuple-element.83, ...), kind=kOutput, calls=%fused_computation.38 | convolution fusion | flops 2156396544 | bytes 10485760 | tf_op jit(solution)/shard_map/dot_general | solution.py:108
  159.0 1.5 collective-permute-done.19
  160.5 1.5 collective-permute-start.42
  163.0 23.5 %collective-permute-done.27 = bf16[128,2048]{1,0:T(8,128)(2,1)S(1)} collective-permute-done((bf16[128,2048]{1,0:T(8,128)(2,1)S(1)}, bf16[128,2048]{1,0:T(8,128)(2,1)S(1)}, u32[]{:S(2)}, u32[]{:S(2)}) %collective-permute-start.27) | collective-permute-done | bytes 524320 | tf_op jit(solution)/shard_map/ppermute | solution.py:146
  186.7 1.7 collective-permute-done.28
  188.4 2.4 convolution_convert_fusion.1
  190.9 0.8 pad_maximum_fusion.7
  191.8 0.8 slice.360
  193.4 1.3 collective-permute-start.31
  194.7 1.1 fusion.54
  196.6 1.1 constant_dynamic-slice_fusion.16
  198.4 14.6 %collective-permute-done.43 = bf16[256,512]{1,0:T(8,128)(2,1)} collective-permute-done((bf16[256,512]{1,0:T(8,128)(2,1)}, bf16[256,512]{1,0:T(8,128)(2,1)}, u32[]{:S(2)}, u32[]{:S(2)}) %collective-permute-start.43) | collective-permute-done | bytes 262176 | tf_op jit(solution)/shard_map/ppermute | solution.py:18
  213.0 1.2 fusion.57
  214.2 1.3 fusion.51
  215.5 1.4 collective-permute-start.30
  216.9 1.5 collective-permute-start.32
  218.4 5.7 %fusion.35 = f32[1024,512]{1,0:T(8,128)S(1)} fusion(f32[1024,512]{1,0:T(8,128)} %fusion.38, bf16[1024,2048]{1,0:T(8,128)(2,1)} %copy-done.18, bf16[512,512]{1,0:T(8,128)(2,1)} %get-tuple-element.117, bf16[512,512]{1,0:T(8,128)(2,1)} %get-tuple-element.126, bf16[512,512]{1,0:T(8,128)(2,1)S(1)} %copy-done.11, bf16[512,512]{1,0:T(8,128)(2,1)} %get-tuple-element.79), kind=kOutput, calls=%fused_computation.37 | convolution fusion | flops 2156396544 | bytes 10485760 | tf_op jit(solution)/shard_map/dot_general | solution.py:108
  224.1 3.7 %collective-permute-done.38 = bf16[128,2048]{1,0:T(8,128)(2,1)S(1)} collective-permute-done((bf16[128,2048]{1,0:T(8,128)(2,1)}, bf16[128,2048]{1,0:T(8,128)(2,1)S(1)}, u32[]{:S(2)}, u32[]{:S(2)}) %collective-permute-start.38) | collective-permute-done | bytes 524320 | tf_op jit(solution)/shard_map/ppermute | solution.py:146
  227.8 1.3 collective-permute-start.45
  229.3 1.4 fusion.46
  230.9 1.2 constant_dynamic-update-slice_fusion.29
  232.1 1.1 constant_dynamic-update-slice_fusion.27
  233.4 2.4 convolution_convert_fusion
  236.0 2.3 fusion.32
  238.6 11.4 %attention_grads.1 = (bf16[1024,512]{1,0:T(8,128)(2,1)}, f32[1024,128]{1,0:T(8,128)S(1)}, f32[1024,128]{1,0:T(8,128)S(1)}) custom-call(bf16[1024,512]{1,0:T(8,128)(2,1)S(1)} %copy-done.1, bf16[1024,128]{1,0:T(8,128)(2,1)S(1)} %get-tuple-element.131.k_ref, bf16[128,1024]{1,0:T(8,128)(2,1)S(1)} %bitcast.83, bf16[1024,128]{1,0:T(8,128)(2,1)S(1)} %get-tuple-element.130.v_ref, ...), custom_call_target="tpu_custom_call" | custom-call | flops 5368709120 | bytes 5242880 | tf_op jit(solution)/shard_map/attention_grads/pallas_call | solution.py:70
  250.3 1.1 fusion.58
  251.4 0.8 collective-permute-start.46
  252.2 1.3 collective-permute-start.48
  253.6 10.9 %collective-permute-done.40 = bf16[2,1024,64]{2,1,0:T(8,128)(2,1)S(1)} collective-permute-done((bf16[2,1024,64]{2,1,0:T(8,128)(2,1)S(1)}, bf16[2,1024,64]{2,1,0:T(8,128)(2,1)S(1)}, u32[]{:S(2)}, u32[]{:S(2)}) %collective-permute-start.40) | collective-permute-done | bytes 262176 | tf_op jit(solution)/shard_map/ppermute | solution.py:18
  266.3 1.4 collective-permute-start.47
  268.0 1.6 collective-permute-start.49
  271.1 2.9 %collective-permute-done.47 = bf16[256,512]{1,0:T(8,128)(2,1)S(1)} collective-permute-done((bf16[256,512]{1,0:T(8,128)(2,1)S(1)}, bf16[256,512]{1,0:T(8,128)(2,1)S(1)}, u32[]{:S(2)}, u32[]{:S(2)}) %collective-permute-start.47) | collective-permute-done | bytes 262176 | tf_op jit(solution)/shard_map/ppermute | solution.py:18
  274.0 1.8 fusion.59
  275.8 1.8 fusion.60
  (182 shorter events, 15.3 us)
Async XLA Ops:
  0.6 12.0 %copy-start = (bf16[1024,512]{1,0:T(8,128)(2,1)S(1)}, bf16[1024,512]{1,0:T(8,128)(2,1)}, u32[]{:S(2)}) copy-start(bf16[1024,512]{1,0:T(8,128)(2,1)} %o_ref.1) | copy-start | bytes 3145732
  0.6 62.5 %collective-permute-start.4 = (bf16[2048,512]{1,0:T(8,128)(2,1)}, bf16[2048,512]{1,0:T(8,128)(2,1)S(1)}, u32[]{:S(2)}, u32[]{:S(2)}) collective-permute-start(bf16[2048,512]{1,0:T(8,128)(2,1)} %param.8), channel_id=1, source_target_pairs={{0,8},{8,0},{16,24},{24,16},{1,9},{9,1},{17,25},{25,17},{2,10},{10... | collective-permute-start | bytes 6291464 | tf_op jit(solution)/shard_map/ppermute | solution.py:18
  3.7 60.0 %collective-permute-start.5 = (bf16[2048,512]{1,0:T(8,128)(2,1)}, bf16[2048,512]{1,0:T(8,128)(2,1)}, u32[]{:S(2)}, u32[]{:S(2)}) collective-permute-start(bf16[2048,512]{1,0:T(8,128)(2,1)} %param.8), channel_id=1, source_target_pairs={{0,16},{8,24},{16,0},{24,8},{1,17},{9,25},{17,1},{25,9},{2,18},{10... | collective-permute-start | bytes 6291464 | tf_op jit(solution)/shard_map/ppermute | solution.py:18
  8.6 56.1 %collective-permute-start.6 = (bf16[128,2048]{1,0:T(8,128)(2,1)}, bf16[128,2048]{1,0:T(8,128)(2,1)}, u32[]{:S(2)}, u32[]{:S(2)}) collective-permute-start(bf16[128,2048]{1,0:T(8,128)(2,1)} %pad_maximum_fusion.4), channel_id=1, source_target_pairs={{0,1},{1,0},{2,3},{3,2},{4,5},{5,4},{6,7},{7,6},{8,9},{9,8},{10,11... | collective-permute-start | bytes 1572872 | tf_op jit(solution)/shard_map/ppermute | solution.py:18
  8.6 27.8 %collective-permute-start.2 = (bf16[128,2048]{1,0:T(8,128)(2,1)}, bf16[128,2048]{1,0:T(8,128)(2,1)}, u32[]{:S(2)}, u32[]{:S(2)}) collective-permute-start(bf16[128,2048]{1,0:T(8,128)(2,1)} %pad_maximum_fusion.4), channel_id=1, source_target_pairs={{0,2},{1,3},{2,4},{3,5},{4,6},{5,7},{6,0},{7,1},{8,10},{9,11},{10,... | collective-permute-start | bytes 1572872 | tf_op jit(solution)/shard_map/ppermute | solution.py:146
  11.0 25.3 %collective-permute-start = (bf16[128,2048]{1,0:T(8,128)(2,1)}, bf16[128,2048]{1,0:T(8,128)(2,1)}, u32[]{:S(2)}, u32[]{:S(2)}) collective-permute-start(bf16[128,2048]{1,0:T(8,128)(2,1)} %pad_maximum_fusion.2), channel_id=1, source_target_pairs={{0,2},{1,3},{2,4},{3,5},{4,6},{5,7},{6,0},{7,1},{8,10},{9,11},{10,... | collective-permute-start | bytes 1572872 | tf_op jit(solution)/shard_map/ppermute | solution.py:146
  12.6 26.3 %copy-start.3 = (bf16[2048,512]{1,0:T(8,128)(2,1)S(1)}, bf16[2048,512]{1,0:T(8,128)(2,1)}, u32[]{:S(2)}) copy-start(bf16[2048,512]{1,0:T(8,128)(2,1)} %param.8) | copy-start | bytes 6291460
  12.8 175.6 %copy-start.20 = (bf16[1024,512]{1,0:T(8,128)(2,1)}, bf16[1024,512]{1,0:T(8,128)(2,1)S(1)}, u32[]{:S(2)}) copy-start(bf16[1024,512]{1,0:T(8,128)(2,1)S(1)} %dynamic-slice_dynamic-update-slice_fusion) | copy-start | bytes 3145732
  36.3 16.8 %collective-permute-start.1 = (bf16[128,2048]{1,0:T(8,128)(2,1)}, bf16[128,2048]{1,0:T(8,128)(2,1)S(1)}, u32[]{:S(2)}, u32[]{:S(2)}) collective-permute-start(bf16[128,2048]{1,0:T(8,128)(2,1)} %collective-permute-done), channel_id=1, source_target_pairs={{0,2},{1,3},{2,4},{3,5},{4,6},{5,7},{6,0},{7,1},{8,10},{9,11},{10,... | collective-permute-start | bytes 1572872 | tf_op jit(solution)/shard_map/ppermute | solution.py:146
  36.3 26.8 %collective-permute-start.3 = (bf16[128,2048]{1,0:T(8,128)(2,1)}, bf16[128,2048]{1,0:T(8,128)(2,1)S(1)}, u32[]{:S(2)}, u32[]{:S(2)}) collective-permute-start(bf16[128,2048]{1,0:T(8,128)(2,1)} %collective-permute-done.2), channel_id=1, source_target_pairs={{0,2},{1,3},{2,4},{3,5},{4,6},{5,7},{6,0},{7,1},{8,10},{9,11},{10,... | collective-permute-start | bytes 1572872 | tf_op jit(solution)/shard_map/ppermute | solution.py:146
  38.9 70.3 %copy-start.7 = (bf16[128,2048]{1,0:T(8,128)(2,1)}, bf16[128,2048]{1,0:T(8,128)(2,1)S(1)}, u32[]{:S(2)}) copy-start(bf16[128,2048]{1,0:T(8,128)(2,1)S(1)} %get-tuple-element.52) | copy-start | bytes 1572868
  53.1 54.8 %collective-permute-start.13 = (bf16[128,2048]{1,0:T(8,128)(2,1)}, bf16[128,2048]{1,0:T(8,128)(2,1)S(1)}, u32[]{:S(2)}, u32[]{:S(2)}) collective-permute-start(bf16[128,2048]{1,0:T(8,128)(2,1)} %pad_maximum_fusion.2), channel_id=1, source_target_pairs={{0,1},{1,0},{2,3},{3,2},{4,5},{5,4},{6,7},{7,6},{8,9},{9,8},{10,11... | collective-permute-start | bytes 1572872 | tf_op jit(solution)/shard_map/ppermute | solution.py:18
  63.1 46.1 %collective-permute-start.14 = (bf16[128,2048]{1,0:T(8,128)(2,1)}, bf16[128,2048]{1,0:T(8,128)(2,1)S(1)}, u32[]{:S(2)}, u32[]{:S(2)}) collective-permute-start(bf16[128,2048]{1,0:T(8,128)(2,1)} %collective-permute-done), channel_id=1, source_target_pairs={{0,1},{1,0},{2,3},{3,2},{4,5},{5,4},{6,7},{7,6},{8,9},{9,8},{10,11... | collective-permute-start | bytes 1572872 | tf_op jit(solution)/shard_map/ppermute | solution.py:18
  63.1 3.9 %collective-permute-start.7 = (bf16[128,2048]{1,0:T(8,128)(2,1)}, bf16[128,2048]{1,0:T(8,128)(2,1)S(1)}, u32[]{:S(2)}, u32[]{:S(2)}) collective-permute-start(bf16[128,2048]{1,0:T(8,128)(2,1)} %collective-permute-done.2), channel_id=1, source_target_pairs={{0,1},{1,0},{2,3},{3,2},{4,5},{5,4},{6,7},{7,6},{8,9},{9,8},{10,11... | collective-permute-start | bytes 1572872 | tf_op jit(solution)/shard_map/ppermute | solution.py:18
  63.6 15.7 %collective-permute-start.9 = (bf16[128,2048]{1,0:T(8,128)(2,1)S(1)}, bf16[128,2048]{1,0:T(8,128)(2,1)S(1)}, u32[]{:S(2)}, u32[]{:S(2)}) collective-permute-start(bf16[128,2048]{1,0:T(8,128)(2,1)S(1)} %collective-permute-done.3), channel_id=1, source_target_pairs={{0,2},{1,3},{2,4},{3,5},{4,6},{5,7},{6,0},{7,1},{8,10},{9,11},{10,... | collective-permute-start | bytes 1572872 | tf_op jit(solution)/shard_map/ppermute | solution.py:146
  64.7 16.1 %collective-permute-start.8 = (bf16[128,2048]{1,0:T(8,128)(2,1)S(1)}, bf16[128,2048]{1,0:T(8,128)(2,1)S(1)}, u32[]{:S(2)}, u32[]{:S(2)}) collective-permute-start(bf16[128,2048]{1,0:T(8,128)(2,1)S(1)} %collective-permute-done.3), channel_id=1, source_target_pairs={{0,1},{1,0},{2,3},{3,2},{4,5},{5,4},{6,7},{7,6},{8,9},{9,8},{10,11... | collective-permute-start | bytes 1572872 | tf_op jit(solution)/shard_map/ppermute | solution.py:18
  67.1 95.2 %collective-permute-start.22 = (bf16[128,2048]{1,0:T(8,128)(2,1)S(1)}, bf16[128,2048]{1,0:T(8,128)(2,1)S(1)}, u32[]{:S(2)}, u32[]{:S(2)}) collective-permute-start(bf16[128,2048]{1,0:T(8,128)(2,1)S(1)} %get-tuple-element.47), channel_id=1, source_target_pairs={{0,1},{1,0},{2,3},{3,2},{4,5},{5,4},{6,7},{7,6},{8,9},{9,8},{10,11... | collective-permute-start | bytes 1572872 | tf_op jit(solution)/shard_map/ppermute | solution.py:18
  79.3 2.2 collective-permute-start.10
  80.8 25.6 %collective-permute-start.11 = (bf16[1024,512]{1,0:T(8,128)(2,1)S(1)}, bf16[1024,512]{1,0:T(8,128)(2,1)S(1)}, u32[]{:S(2)}, u32[]{:S(2)}) collective-permute-start(bf16[1024,512]{1,0:T(8,128)(2,1)S(1)} %slice.269), channel_id=1, source_target_pairs={{0,8},{8,0},{16,24},{24,16},{1,9},{9,1},{17,25},{25,17},{2,10},{10... | collective-permute-start | bytes 3145736 | tf_op jit(solution)/shard_map/ppermute | solution.py:18
  81.5 25.4 %collective-permute-start.12 = (bf16[1024,512]{1,0:T(8,128)(2,1)S(1)}, bf16[1024,512]{1,0:T(8,128)(2,1)S(1)}, u32[]{:S(2)}, u32[]{:S(2)}) collective-permute-start(bf16[1024,512]{1,0:T(8,128)(2,1)S(1)} %slice.270), channel_id=1, source_target_pairs={{0,16},{8,24},{16,0},{24,8},{1,17},{9,25},{17,1},{25,9},{2,18},{10... | collective-permute-start | bytes 3145736 | tf_op jit(solution)/shard_map/ppermute | solution.py:18
  84.7 109.9 %copy-start.4 = (bf16[2048,512]{1,0:T(8,128)(2,1)}, bf16[2048,512]{1,0:T(8,128)(2,1)S(1)}, u32[]{:S(2)}) copy-start(bf16[2048,512]{1,0:T(8,128)(2,1)S(1)} %convolution_convert_fusion.3) | copy-start | bytes 6291460
  106.4 27.8 %collective-permute-start.23 = (bf16[128,2048]{1,0:T(8,128)(2,1)S(1)}, bf16[128,2048]{1,0:T(8,128)(2,1)S(1)}, u32[]{:S(2)}, u32[]{:S(2)}) collective-permute-start(bf16[128,2048]{1,0:T(8,128)(2,1)S(1)} %get-tuple-element.47), channel_id=1, source_target_pairs={{0,2},{1,3},{2,4},{3,5},{4,6},{5,7},{6,0},{7,1},{8,10},{9,11},{10,... | collective-permute-start | bytes 1572872 | tf_op jit(solution)/shard_map/ppermute | solution.py:146
  106.9 27.4 %collective-permute-start.16 = (bf16[128,2048]{1,0:T(8,128)(2,1)S(1)}, bf16[128,2048]{1,0:T(8,128)(2,1)S(1)}, u32[]{:S(2)}, u32[]{:S(2)}) collective-permute-start(bf16[128,2048]{1,0:T(8,128)(2,1)S(1)} %collective-permute-done.1), channel_id=1, source_target_pairs={{0,2},{1,3},{2,4},{3,5},{4,6},{5,7},{6,0},{7,1},{8,10},{9,11},{10,... | collective-permute-start | bytes 1572872 | tf_op jit(solution)/shard_map/ppermute | solution.py:146
  108.0 26.4 %collective-permute-start.15 = (bf16[128,2048]{1,0:T(8,128)(2,1)S(1)}, bf16[128,2048]{1,0:T(8,128)(2,1)S(1)}, u32[]{:S(2)}, u32[]{:S(2)}) collective-permute-start(bf16[128,2048]{1,0:T(8,128)(2,1)S(1)} %collective-permute-done.1), channel_id=1, source_target_pairs={{0,1},{1,0},{2,3},{3,2},{4,5},{5,4},{6,7},{7,6},{8,9},{9,8},{10,11... | collective-permute-start | bytes 1572872 | tf_op jit(solution)/shard_map/ppermute | solution.py:18
  109.2 49.7 %collective-permute-start.34 = (bf16[128,2048]{1,0:T(8,128)(2,1)S(1)}, bf16[128,2048]{1,0:T(8,128)(2,1)}, u32[]{:S(2)}, u32[]{:S(2)}) collective-permute-start(bf16[128,2048]{1,0:T(8,128)(2,1)S(1)} %get-tuple-element.52), channel_id=1, source_target_pairs={{0,2},{1,3},{2,4},{3,5},{4,6},{5,7},{6,0},{7,1},{8,10},{9,11},{10,... | collective-permute-start | bytes 1572872 | tf_op jit(solution)/shard_map/ppermute | solution.py:146
  134.3 1.9 collective-permute-start.17
  134.3 24.6 %collective-permute-start.25 = (bf16[128,2048]{1,0:T(8,128)(2,1)S(1)}, bf16[128,2048]{1,0:T(8,128)(2,1)S(1)}, u32[]{:S(2)}, u32[]{:S(2)}) collective-permute-start(bf16[128,2048]{1,0:T(8,128)(2,1)S(1)} %collective-permute-done.23), channel_id=1, source_target_pairs={{0,2},{1,3},{2,4},{3,5},{4,6},{5,7},{6,0},{7,1},{8,10},{9,11},{10,... | collective-permute-start | bytes 1572872 | tf_op jit(solution)/shard_map/ppermute | solution.py:146
  138.8 14.0 %collective-permute-start.18 = (bf16[2,256,512]{2,1,0:T(8,128)(2,1)S(1)}, bf16[2,256,512]{2,1,0:T(8,128)(2,1)S(1)}, u32[]{:S(2)}, u32[]{:S(2)}) collective-permute-start(bf16[2,256,512]{2,1,0:T(8,128)(2,1)S(1)} %pad_maximum_fusion.5), channel_id=1, source_target_pairs={{0,8},{8,0},{16,24},{24,16},{1,9},{9,1},{17,25},{25,17},{2,10},{10... | collective-permute-start | bytes 1572872 | tf_op jit(solution)/shard_map/ppermute | solution.py:18
  139.4 13.7 %collective-permute-start.20 = (bf16[2,256,512]{2,1,0:T(8,128)(2,1)S(1)}, bf16[2,256,512]{2,1,0:T(8,128)(2,1)S(1)}, u32[]{:S(2)}, u32[]{:S(2)}) collective-permute-start(bf16[2,256,512]{2,1,0:T(8,128)(2,1)S(1)} %slice.349), channel_id=1, source_target_pairs={{0,16},{8,24},{16,0},{24,8},{1,17},{9,25},{17,1},{25,9},{2,18},{10... | collective-permute-start | bytes 1572872 | tf_op jit(solution)/shard_map/ppermute | solution.py:18
  153.2 7.3 %collective-permute-start.19 = (bf16[256,512]{1,0:T(8,128)(2,1)S(1)}, bf16[256,512]{1,0:T(8,128)(2,1)S(1)}, u32[]{:S(2)}, u32[]{:S(2)}) collective-permute-start(bf16[256,512]{1,0:T(8,128)(2,1)S(1)} %get-tuple-element.96), channel_id=1, source_target_pairs={{0,16},{8,24},{16,0},{24,8},{1,17},{9,25},{17,1},{25,9},{2,18},{10... | collective-permute-start | bytes 786440 | tf_op jit(solution)/shard_map/ppermute | solution.py:18
  154.0 8.0 %collective-permute-start.21 = (bf16[256,512]{1,0:T(8,128)(2,1)S(1)}, bf16[256,512]{1,0:T(8,128)(2,1)S(1)}, u32[]{:S(2)}, u32[]{:S(2)}) collective-permute-start(bf16[256,512]{1,0:T(8,128)(2,1)S(1)} %get-tuple-element.97), channel_id=1, source_target_pairs={{0,8},{8,0},{16,24},{24,16},{1,9},{9,1},{17,25},{25,17},{2,10},{10... | collective-permute-start | bytes 786440 | tf_op jit(solution)/shard_map/ppermute | solution.py:18
  158.9 3.6 %collective-permute-start.24 = (bf16[128,2048]{1,0:T(8,128)(2,1)S(1)}, bf16[128,2048]{1,0:T(8,128)(2,1)S(1)}, u32[]{:S(2)}, u32[]{:S(2)}) collective-permute-start(bf16[128,2048]{1,0:T(8,128)(2,1)S(1)} %collective-permute-done.23), channel_id=1, source_target_pairs={{0,1},{1,0},{2,3},{3,2},{4,5},{5,4},{6,7},{7,6},{8,9},{9,8},{10,11... | collective-permute-start | bytes 1572872 | tf_op jit(solution)/shard_map/ppermute | solution.py:18
  158.9 39.0 %collective-permute-start.36 = (bf16[128,2048]{1,0:T(8,128)(2,1)}, bf16[128,2048]{1,0:T(8,128)(2,1)}, u32[]{:S(2)}, u32[]{:S(2)}) collective-permute-start(bf16[128,2048]{1,0:T(8,128)(2,1)} %collective-permute-done.34), channel_id=1, source_target_pairs={{0,2},{1,3},{2,4},{3,5},{4,6},{5,7},{6,0},{7,1},{8,10},{9,11},{10,... | collective-permute-start | bytes 1572872 | tf_op jit(solution)/shard_map/ppermute | solution.py:146
  160.5 34.2 %collective-permute-start.42 = (bf16[2,256,512]{2,1,0:T(8,128)(2,1)S(1)}, bf16[2,256,512]{2,1,0:T(8,128)(2,1)S(1)}, u32[]{:S(2)}, u32[]{:S(2)}) collective-permute-start(bf16[2,256,512]{2,1,0:T(8,128)(2,1)S(1)} %pad_maximum_fusion.10), channel_id=1, source_target_pairs={{0,8},{8,0},{16,24},{24,16},{1,9},{9,1},{17,25},{25,17},{2,10},{10... | collective-permute-start | bytes 1572872 | tf_op jit(solution)/shard_map/ppermute | solution.py:18
  162.0 24.5 %collective-permute-start.27 = (bf16[128,2048]{1,0:T(8,128)(2,1)S(1)}, bf16[128,2048]{1,0:T(8,128)(2,1)S(1)}, u32[]{:S(2)}, u32[]{:S(2)}) collective-permute-start(bf16[128,2048]{1,0:T(8,128)(2,1)S(1)} %collective-permute-done.25), channel_id=1, source_target_pairs={{0,2},{1,3},{2,4},{3,5},{4,6},{5,7},{6,0},{7,1},{8,10},{9,11},{10,... | collective-permute-start | bytes 1572872 | tf_op jit(solution)/shard_map/ppermute | solution.py:146
  162.3 24.3 %collective-permute-start.26 = (bf16[128,2048]{1,0:T(8,128)(2,1)S(1)}, bf16[128,2048]{1,0:T(8,128)(2,1)S(1)}, u32[]{:S(2)}, u32[]{:S(2)}) collective-permute-start(bf16[128,2048]{1,0:T(8,128)(2,1)S(1)} %collective-permute-done.25), channel_id=1, source_target_pairs={{0,1},{1,0},{2,3},{3,2},{4,5},{5,4},{6,7},{7,6},{8,9},{9,8},{10,11... | collective-permute-start | bytes 1572872 | tf_op jit(solution)/shard_map/ppermute | solution.py:18
  162.5 32.2 %collective-permute-start.44 = (bf16[2,256,512]{2,1,0:T(8,128)(2,1)S(1)}, bf16[2,256,512]{2,1,0:T(8,128)(2,1)S(1)}, u32[]{:S(2)}, u32[]{:S(2)}) collective-permute-start(bf16[2,256,512]{2,1,0:T(8,128)(2,1)S(1)} %slice.388), channel_id=1, source_target_pairs={{0,16},{8,24},{16,0},{24,8},{1,17},{9,25},{17,1},{25,9},{2,18},{10... | collective-permute-start | bytes 1572872 | tf_op jit(solution)/shard_map/ppermute | solution.py:18
  186.5 1.9 collective-permute-start.28
  190.8 4.9 %copy-start.5 = (bf16[2048,512]{1,0:T(8,128)(2,1)}, bf16[2048,512]{1,0:T(8,128)(2,1)S(1)}, u32[]{:S(2)}) copy-start(bf16[2048,512]{1,0:T(8,128)(2,1)S(1)} %convolution_convert_fusion.1) | copy-start | bytes 6291460
  190.9 7.0 %copy-start.8 = (bf16[128,2048]{1,0:T(8,128)(2,1)S(1)}, bf16[128,2048]{1,0:T(8,128)(2,1)}, u32[]{:S(2)}) copy-start(bf16[128,2048]{1,0:T(8,128)(2,1)} %copy-done.7) | copy-start | bytes 1572868
  190.9 27.5 %copy-start.11 = (bf16[512,512]{1,0:T(8,128)(2,1)S(1)}, bf16[512,512]{1,0:T(8,128)(2,1)}, u32[]{:S(2)}) copy-start(bf16[512,512]{1,0:T(8,128)(2,1)} %get-tuple-element.81) | copy-start | bytes 1572868
  192.6 21.6 %collective-permute-start.29 = (bf16[2,256,512]{2,1,0:T(8,128)(2,1)}, bf16[2,256,512]{2,1,0:T(8,128)(2,1)}, u32[]{:S(2)}, u32[]{:S(2)}) collective-permute-start(bf16[2,256,512]{2,1,0:T(8,128)(2,1)} %pad_maximum_fusion.7), channel_id=1, source_target_pairs={{0,8},{8,0},{16,24},{24,16},{1,9},{9,1},{17,25},{25,17},{2,10},{10... | collective-permute-start | bytes 1572872 | tf_op jit(solution)/shard_map/ppermute | solution.py:18
  193.4 20.8 %collective-permute-start.31 = (bf16[2,256,512]{2,1,0:T(8,128)(2,1)}, bf16[2,256,512]{2,1,0:T(8,128)(2,1)}, u32[]{:S(2)}, u32[]{:S(2)}) collective-permute-start(bf16[2,256,512]{2,1,0:T(8,128)(2,1)} %slice.360), channel_id=1, source_target_pairs={{0,16},{8,24},{16,0},{24,8},{1,17},{9,25},{17,1},{25,9},{2,18},{10... | collective-permute-start | bytes 1572872 | tf_op jit(solution)/shard_map/ppermute | solution.py:18
  195.8 17.2 %collective-permute-start.43 = (bf16[256,512]{1,0:T(8,128)(2,1)}, bf16[256,512]{1,0:T(8,128)(2,1)}, u32[]{:S(2)}, u32[]{:S(2)}) collective-permute-start(bf16[256,512]{1,0:T(8,128)(2,1)} %get-tuple-element.71), channel_id=1, source_target_pairs={{0,16},{8,24},{16,0},{24,8},{1,17},{9,25},{17,1},{25,9},{2,18},{10... | collective-permute-start | bytes 786440 | tf_op jit(solution)/shard_map/ppermute | solution.py:18
  197.8 33.0 %collective-permute-start.33 = (bf16[128,2048]{1,0:T(8,128)(2,1)S(1)}, bf16[128,2048]{1,0:T(8,128)(2,1)S(1)}, u32[]{:S(2)}, u32[]{:S(2)}) collective-permute-start(bf16[128,2048]{1,0:T(8,128)(2,1)S(1)} %copy-done.8), channel_id=1, source_target_pairs={{0,1},{1,0},{2,3},{3,2},{4,5},{5,4},{6,7},{7,6},{8,9},{9,8},{10,11... | collective-permute-start | bytes 1572872 | tf_op jit(solution)/shard_map/ppermute | solution.py:18
  197.9 34.1 %collective-permute-start.35 = (bf16[128,2048]{1,0:T(8,128)(2,1)}, bf16[128,2048]{1,0:T(8,128)(2,1)S(1)}, u32[]{:S(2)}, u32[]{:S(2)}) collective-permute-start(bf16[128,2048]{1,0:T(8,128)(2,1)} %collective-permute-done.34), channel_id=1, source_target_pairs={{0,1},{1,0},{2,3},{3,2},{4,5},{5,4},{6,7},{7,6},{8,9},{9,8},{10,11... | collective-permute-start | bytes 1572872 | tf_op jit(solution)/shard_map/ppermute | solution.py:18
  213.0 14.8 %collective-permute-start.38 = (bf16[128,2048]{1,0:T(8,128)(2,1)}, bf16[128,2048]{1,0:T(8,128)(2,1)S(1)}, u32[]{:S(2)}, u32[]{:S(2)}) collective-permute-start(bf16[128,2048]{1,0:T(8,128)(2,1)} %collective-permute-done.36), channel_id=1, source_target_pairs={{0,2},{1,3},{2,4},{3,5},{4,6},{5,7},{6,0},{7,1},{8,10},{9,11},{10,... | collective-permute-start | bytes 1572872 | tf_op jit(solution)/shard_map/ppermute | solution.py:146
  215.5 12.3 %collective-permute-start.30 = (bf16[256,512]{1,0:T(8,128)(2,1)S(1)}, bf16[256,512]{1,0:T(8,128)(2,1)S(1)}, u32[]{:S(2)}, u32[]{:S(2)}) collective-permute-start(bf16[256,512]{1,0:T(8,128)(2,1)S(1)} %get-tuple-element.90), channel_id=1, source_target_pairs={{0,16},{8,24},{16,0},{24,8},{1,17},{9,25},{17,1},{25,9},{2,18},{10... | collective-permute-start | bytes 786440 | tf_op jit(solution)/shard_map/ppermute | solution.py:18
  216.9 12.3 %collective-permute-start.32 = (bf16[256,512]{1,0:T(8,128)(2,1)S(1)}, bf16[256,512]{1,0:T(8,128)(2,1)S(1)}, u32[]{:S(2)}, u32[]{:S(2)}) collective-permute-start(bf16[256,512]{1,0:T(8,128)(2,1)S(1)} %get-tuple-element.91), channel_id=1, source_target_pairs={{0,8},{8,0},{16,24},{24,16},{1,9},{9,1},{17,25},{25,17},{2,10},{10... | collective-permute-start | bytes 786440 | tf_op jit(solution)/shard_map/ppermute | solution.py:18
  218.4 9.4 %copy-start.17 = (bf16[256,512]{1,0:T(8,128)(2,1)S(1)}, bf16[256,512]{1,0:T(8,128)(2,1)}, u32[]{:S(2)}) copy-start(bf16[256,512]{1,0:T(8,128)(2,1)} %get-tuple-element.70) | copy-start | bytes 786436
  227.8 5.4 %collective-permute-start.37 = (bf16[128,2048]{1,0:T(8,128)(2,1)}, bf16[128,2048]{1,0:T(8,128)(2,1)S(1)}, u32[]{:S(2)}, u32[]{:S(2)}) collective-permute-start(bf16[128,2048]{1,0:T(8,128)(2,1)} %collective-permute-done.36), channel_id=1, source_target_pairs={{0,1},{1,0},{2,3},{3,2},{4,5},{5,4},{6,7},{7,6},{8,9},{9,8},{10,11... | collective-permute-start | bytes 1572872 | tf_op jit(solution)/shard_map/ppermute | solution.py:18
  227.8 22.5 %collective-permute-start.45 = (bf16[256,512]{1,0:T(8,128)(2,1)S(1)}, bf16[256,512]{1,0:T(8,128)(2,1)S(1)}, u32[]{:S(2)}, u32[]{:S(2)}) collective-permute-start(bf16[256,512]{1,0:T(8,128)(2,1)S(1)} %copy-done.17), channel_id=1, source_target_pairs={{0,8},{8,0},{16,24},{24,16},{1,9},{9,1},{17,25},{25,17},{2,10},{10... | collective-permute-start | bytes 786440 | tf_op jit(solution)/shard_map/ppermute | solution.py:18
  229.2 4.1 %collective-permute-start.39 = (bf16[128,2048]{1,0:T(8,128)(2,1)S(1)}, bf16[128,2048]{1,0:T(8,128)(2,1)S(1)}, u32[]{:S(2)}, u32[]{:S(2)}) collective-permute-start(bf16[128,2048]{1,0:T(8,128)(2,1)S(1)} %collective-permute-done.38), channel_id=1, source_target_pairs={{0,1},{1,0},{2,3},{3,2},{4,5},{5,4},{6,7},{7,6},{8,9},{9,8},{10,11... | collective-permute-start | bytes 1572872 | tf_op jit(solution)/shard_map/ppermute | solution.py:18
  235.8 30.4 %copy-start.6 = (bf16[2048,512]{1,0:T(8,128)(2,1)}, bf16[2048,512]{1,0:T(8,128)(2,1)S(1)}, u32[]{:S(2)}) copy-start(bf16[2048,512]{1,0:T(8,128)(2,1)S(1)} %convolution_convert_fusion) | copy-start | bytes 6291460
  236.0 2.6 copy-start.1
  236.0 2.6 copy-start.2
  238.6 11.7 %copy-start.13 = (bf16[2,256,512]{2,1,0:T(8,128)(2,1)S(1)}, bf16[2,256,512]{2,1,0:T(8,128)(2,1)}, u32[]{:S(2)}) copy-start(bf16[2,256,512]{2,1,0:T(8,128)(2,1)} %copy-done.12) | copy-start | bytes 1572868
  250.2 14.2 %collective-permute-start.40 = (bf16[2,1024,64]{2,1,0:T(8,128)(2,1)S(1)}, bf16[2,1024,64]{2,1,0:T(8,128)(2,1)S(1)}, u32[]{:S(2)}, u32[]{:S(2)}) collective-permute-start(bf16[2,1024,64]{2,1,0:T(8,128)(2,1)S(1)} %select_convert_fusion.1), channel_id=1, source_target_pairs={{0,2},{1,3},{2,0},{3,1},{4,6},{5,7},{6,4},{7,5},{8,10},{9,11},{10,... | collective-permute-start | bytes 786440 | tf_op jit(solution)/shard_map/ppermute | solution.py:18
  251.4 14.2 %collective-permute-start.46 = (bf16[2,256,512]{2,1,0:T(8,128)(2,1)S(1)}, bf16[2,256,512]{2,1,0:T(8,128)(2,1)S(1)}, u32[]{:S(2)}, u32[]{:S(2)}) collective-permute-start(bf16[2,256,512]{2,1,0:T(8,128)(2,1)S(1)} %pad_maximum_fusion.9), channel_id=1, source_target_pairs={{0,8},{8,0},{16,24},{24,16},{1,9},{9,1},{17,25},{25,17},{2,10},{10... | collective-permute-start | bytes 1572872 | tf_op jit(solution)/shard_map/ppermute | solution.py:18
  252.2 13.9 %collective-permute-start.48 = (bf16[2,256,512]{2,1,0:T(8,128)(2,1)S(1)}, bf16[2,256,512]{2,1,0:T(8,128)(2,1)S(1)}, u32[]{:S(2)}, u32[]{:S(2)}) collective-permute-start(bf16[2,256,512]{2,1,0:T(8,128)(2,1)S(1)} %slice.366), channel_id=1, source_target_pairs={{0,16},{8,24},{16,0},{24,8},{1,17},{9,25},{17,1},{25,9},{2,18},{10... | collective-permute-start | bytes 1572872 | tf_op jit(solution)/shard_map/ppermute | solution.py:18
  253.6 14.4 %copy-start.19 = (bf16[2048,512]{1,0:T(8,128)(2,1)}, bf16[2048,512]{1,0:T(8,128)(2,1)S(1)}, u32[]{:S(2)}) copy-start(bf16[2048,512]{1,0:T(8,128)(2,1)S(1)} %constant_dynamic-update-slice_fusion.32) | copy-start | bytes 6291460
  265.0 2.6 collective-permute-start.41
  266.3 7.7 %collective-permute-start.47 = (bf16[256,512]{1,0:T(8,128)(2,1)S(1)}, bf16[256,512]{1,0:T(8,128)(2,1)S(1)}, u32[]{:S(2)}, u32[]{:S(2)}) collective-permute-start(bf16[256,512]{1,0:T(8,128)(2,1)S(1)} %get-tuple-element.69), channel_id=1, source_target_pairs={{0,16},{8,24},{16,0},{24,8},{1,17},{9,25},{17,1},{25,9},{2,18},{10... | collective-permute-start | bytes 786440 | tf_op jit(solution)/shard_map/ppermute | solution.py:18
  268.0 7.8 %collective-permute-start.49 = (bf16[256,512]{1,0:T(8,128)(2,1)S(1)}, bf16[256,512]{1,0:T(8,128)(2,1)S(1)}, u32[]{:S(2)}, u32[]{:S(2)}) collective-permute-start(bf16[256,512]{1,0:T(8,128)(2,1)S(1)} %get-tuple-element.68), channel_id=1, source_target_pairs={{0,8},{8,0},{16,24},{24,16},{1,9},{9,1},{17,25},{25,17},{2,10},{10... | collective-permute-start | bytes 786440 | tf_op jit(solution)/shard_map/ppermute | solution.py:18
  (8 other events, 17.6 us)
where the time goes:
time: 278 us
  waiting for transfers between devices  173 us (62%)
  starting transfers between devices  30.5 us (11%)
  matrix products  23.5 us (8%)
  local copies, waits for them, and re-layouts  22.7 us (8%)
  other arithmetic  15.2 us (5%)
  Pallas kernels  11.4 us (4%)
    ppermute x12, waiting for transfers between devices, projection_chunked(): slots.append(lax.ppermute(slots[-1], 'tensor', ring))  110 us
    ppermute x38, waiting for transfers between devices, partner(): return lax.ppermute(value, axis, pairs)  62.3 us
    ppermute x38, starting transfers between devices, partner(): return lax.ppermute(value, axis, pairs)  25.6 us
    dot_general x4, matrix products, add_term(): term = jnp.dot(chunk, weight, preferred_element_type=jnp.float32)  14 us
    pallas_call x1, Pallas kernels, attention_grads(): pl.pallas_call(functools.partial(attention_kernel, 256), grid=(heads,), i...  11.4 us
    unnamed x84, local copies, waits for them, and re-layouts  10.4 us
    dot_general x4, matrix products, projection_chunked(): lax.dot_general(chunk, attended, (((0,), (0,)), ((), ())), preferred_elem...  9.52 us
  transfers between devices with their start and end apart: 50, of which 19 were waited for; matrix products, arithmetic and copies ran while one was open for 21% of the time, Pallas kernels for 4%

commit v1 on v0

--- a/solution.py
+++ b/solution.py
@@ -22,7 +22,7 @@
     return lax.dot_general(a, b, (((1,), (1,)), ((), ())), preferred_element_type=jnp.float32)
 
 
-def attention_kernel(block, q_ref, k_ref, kt_ref, v_ref, o_ref, g_ref, s_ref, dq_ref, dk_ref, dv_ref):
+def attention_kernel(block, q_ref, k_ref, kt_ref, v_ref, o_ref, g_ref, s_ref, dq_ref, dkt_ref, dvt_ref, dk_ref, dv_ref):
     head = pl.program_id(0)
     length = q_ref.shape[0]
     scale = HD ** (-0.5)
@@ -59,7 +59,8 @@
 
     @pl.when(head == pl.num_programs(0) - 1)
     def _():
-        dk_ref[...] = dk_ref[...] * scale
+        dkt_ref[...] = (dk_ref[...] * scale).T
+        dvt_ref[...] = dv_ref[...].T
 
 
 def attention_grads(query, key_one, value_one, attended, grad_att, stats):
@@ -67,23 +68,25 @@
     heads = width // HD
     per_head = pl.BlockSpec((length, HD), lambda h: (0, h))
     shared = pl.BlockSpec((length, HD), lambda h: (0, 0))
+    flat = pl.BlockSpec((HD, length), lambda h: (0, 0))
     return pl.pallas_call(
         functools.partial(attention_kernel, 256),
         grid=(heads,),
         in_specs=[
             per_head,
             shared,
-            pl.BlockSpec((HD, length), lambda h: (0, 0)),
+            flat,
             shared,
             per_head,
             per_head,
             pl.BlockSpec((heads, length), lambda h: (0, 0)),
         ],
-        out_specs=[per_head, shared, shared],
+        out_specs=[per_head, flat, flat],
+        scratch_shapes=[pltpu.VMEM((length, HD), jnp.float32)] * 2,
         out_shape=[
             jax.ShapeDtypeStruct((length, width), jnp.bfloat16),
-            jax.ShapeDtypeStruct((length, HD), jnp.float32),
-            jax.ShapeDtypeStruct((length, HD), jnp.float32),
+            jax.ShapeDtypeStruct((HD, length), jnp.float32),
+            jax.ShapeDtypeStruct((HD, length), jnp.float32),
         ],
         compiler_params=pltpu.CompilerParams(
             dimension_semantics=("arbitrary",), vmem_limit_bytes=40 * 2**20
@@ -127,64 +130,100 @@
     attended = jnp.concatenate(
         [lax.dynamic_slice_in_dim(attended, h * local, local, 0) for h in order], axis=0
     )
-    total = None
-    parts = []
-    owned = []
-    arrived = []
-    for c in range(CHUNKS):
-        mine = jnp.concatenate(
+    barrier = lax.optimization_barrier
+
+    def cut(c):
+        return jnp.concatenate(
             [
                 lax.dynamic_slice_in_dim(grad_out, (me ^ r) * rows + c * depth, depth, 1)
                 for r in range(dp)
             ],
             axis=1,
         )
-        if c >= 2:
-            mine, arrived[c - 2][-2] = lax.optimization_barrier((mine, arrived[c - 2][-2]))
-        slots = [mine]
-        for _ in range(chips - 1):
-            slots.append(lax.ppermute(slots[-1], "tensor", ring))
-        arrived.append(slots)
-    for c in range(CHUNKS):
-        part = slice(c * depth, (c + 1) * depth)
-        blocks = []
-        for slot in arrived[c]:
-            blocks += [slot, partner(slot, "tensor", 1)]
-        if c == 0:
-            blocks[0], w_x, w_y = lax.optimization_barrier((blocks[0], w_x, w_y))
-        elif c == 1:
-            w_lo = partner(w_y[:half_rows], "dp", 1)
-            w_hi = partner(w_x[half_rows:], "dp", 2)
-            blocks[0], w_lo, w_hi = lax.optimization_barrier((blocks[0], w_lo, w_hi))
-        else:
-            blocks[0], total, owned[-1] = lax.optimization_barrier((blocks[0], total, owned[-1]))
-        chunk = jnp.concatenate(blocks, axis=0)
-        partial = lax.dot_general(
+
+    def hop(slot):
+        return lax.ppermute(slot, "tensor", ring)
+
+    def weight_term(chunk):
+        return lax.dot_general(
             chunk, attended, (((0,), (0,)), ((), ())), preferred_element_type=jnp.float32
         ).astype(jnp.bfloat16)
-        chunk, partial = lax.optimization_barrier((chunk, partial))
+
+    def joined(slots, tie=()):
+        blocks = []
+        for slot in slots:
+            blocks += [slot, partner(slot, "tensor", 1)]
+        blocks[0], *tie = barrier((blocks[0], *tie))
+        return jnp.concatenate(blocks, axis=0), tie
+
+    def sends(partial):
         partial = partial.reshape(dp, depth, -1)
         upper, lower = partial[:, :half_depth], partial[:, half_depth:]
-        send_upper = jnp.stack([upper[1], upper[3]])
-        send_lower = lower[2:4]
-        parts.append((chunk, part))
-        if c >= 1:
-            for done, where in parts:
-                total = add_term(total, done, where, (out_weight, w_x, w_y, w_lo, w_hi))
-            parts = []
-        if c == CHUNKS - 1:
-            total, send_upper, send_lower = lax.optimization_barrier(
-                (total, send_upper, send_lower)
-            )
-        got_upper = partner(send_upper, "dp", 1)
-        got_lower = partner(send_lower, "dp", 2)
-        keep = upper[0].astype(jnp.float32) + got_upper[0].astype(jnp.float32)
-        pass_on = upper[2].astype(jnp.float32) + got_upper[1].astype(jnp.float32)
-        out_upper = keep + partner(pass_on.astype(jnp.bfloat16), "dp", 2).astype(jnp.float32)
-        keep = lower[0].astype(jnp.float32) + got_lower[0].astype(jnp.float32)
-        pass_on = lower[1].astype(jnp.float32) + got_lower[1].astype(jnp.float32)
-        out_lower = keep + partner(pass_on.astype(jnp.bfloat16), "dp", 1).astype(jnp.float32)
-        owned.append(jnp.concatenate([out_upper, out_lower], axis=0).astype(jnp.bfloat16))
+        return upper, lower, jnp.stack([upper[1], upper[3]]), lower[2:4]
+
+    def first(upper, lower):
+        got_upper = partner(upper, "dp", 1)
+        got_lower = partner(lower, "dp", 2)
+        return got_upper, got_lower
+
+    def second(upper, lower, got_upper, got_lower):
+        wide = jnp.float32
+        up = (upper[2].astype(wide) + got_upper[1].astype(wide)).astype(jnp.bfloat16)
+        low = (lower[1].astype(wide) + got_lower[1].astype(wide)).astype(jnp.bfloat16)
+        up = partner(up, "dp", 2)
+        low = partner(low, "dp", 1)
+        up = upper[0].astype(wide) + got_upper[0].astype(wide) + up.astype(wide)
+        low = lower[0].astype(wide) + got_lower[0].astype(wide) + low.astype(wide)
+        return jnp.concatenate([up, low], axis=0).astype(jnp.bfloat16)
+
+    part = [slice(c * depth, (c + 1) * depth) for c in range(CHUNKS)]
+    owned = []
+    total = None
+    late = None
+    for pair in range(0, CHUNKS, 2):
+        one, two = [cut(pair)], [cut(pair + 1)]
+        if late is not None:
+            one[0], late[0][-1] = barrier((one[0], late[0][-1]))
+            two[0], late[1][-1] = barrier((two[0], late[1][-1]))
+            chunk_0, (w_lo, w_hi) = joined(late[0], (w_lo, w_hi))
+            partial = weight_term(chunk_0)
+            chunk_0, partial = barrier((chunk_0, partial))
+            upper, lower, *out = sends(partial)
+            owned.append(second(upper, lower, *first(*out)))
+            chunk_1, _ = joined(late[1])
+            partial = weight_term(chunk_1)
+            chunk_1, partial = barrier((chunk_1, partial))
+            upper, lower, *out = sends(partial)
+            owned.append(second(upper, lower, *first(*out)))
+            weights = (out_weight, w_x, w_y, w_lo, w_hi)
+            total = add_term(total, chunk_0, part[pair - 2], weights)
+            total = add_term(total, chunk_1, part[pair - 1], weights)
+        for step in range(1, chips):
+            if late is not None and step == 2:
+                one[-1], owned[-2] = barrier((one[-1], owned[-2]))
+            if late is not None and step == 3:
+                one[-1], owned[-1] = barrier((one[-1], owned[-1]))
+                two[-1], total = barrier((two[-1], total))
+            if late is None and step == chips - 1:
+                two[-1], w_x, w_y = barrier((two[-1], w_x, w_y))
+                w_lo = partner(w_y[:half_rows], "dp", 1)
+                w_hi = partner(w_x[half_rows:], "dp", 2)
+            one.append(hop(one[-1]))
+            two.append(hop(two[-1]))
+        late = (one, two)
+    chunk_0, _ = joined(late[0])
+    partial = weight_term(chunk_0)
+    chunk_0, partial = barrier((chunk_0, partial))
+    upper, lower, *out = sends(partial)
+    got = first(*out)
+    total = add_term(total, chunk_0, part[-2], weights)
+    chunk_1, (total,) = joined(late[1], (total,))
+    partial = weight_term(chunk_1)
+    chunk_1, partial, *got = barrier((chunk_1, partial, *got))
+    owned.append(second(upper, lower, *got))
+    upper, lower, *out = sends(partial)
+    owned.append(second(upper, lower, *first(*out)))
+    total = add_term(total, chunk_1, part[-1], weights)
     grad_att = total.astype(jnp.bfloat16)
     unrolled = jnp.zeros_like(grad_att)
     for k, h in enumerate(order):
@@ -225,20 +264,18 @@
     )
     group_span = GROUP // heads
     group_place = tensor_index % group_span
-    bit_count = group_span.bit_length() - 1
-    running_kv = jnp.stack([key_part, value_part])
-    for bit_number in reversed(range(bit_count)):
-        half_cols = running_kv.shape[2] // 2
-        lower_cols = running_kv[:, :, :half_cols]
-        upper_cols = running_kv[:, :, half_cols:]
-        upper_half = group_place // (1 << bit_number) % 2 == 1
-        kept_cols = jnp.where(upper_half, upper_cols, lower_cols)
-        sent_cols = jnp.where(upper_half, lower_cols, upper_cols)
-        running_kv = kept_cols + partner(
-            sent_cols.astype(jnp.bfloat16), "tensor", 1 << bit_number
-        ).astype(sent_cols.dtype)
-    key_grad = running_kv[0].astype(jnp.bfloat16)
-    value_grad = running_kv[1].astype(jnp.bfloat16)
+    width, length = HD // group_span, query.shape[0]
+    running_kv = jnp.stack([key_part, value_part]).reshape(2, group_span, width, length)
+    for bit_number in range(group_span.bit_length() - 1):
+        pairs = running_kv.reshape(2, -1, 2, width, length)
+        odd = (group_place >> bit_number) % 2 == 1
+        kept = jnp.where(odd, pairs[:, :, 1], pairs[:, :, 0])
+        sent = jnp.where(odd, pairs[:, :, 0], pairs[:, :, 1])
+        running_kv = kept + partner(
+            sent.astype(jnp.bfloat16), "tensor", 1 << bit_number
+        ).astype(sent.dtype)
+    key_grad = running_kv[0, 0].T.astype(jnp.bfloat16)
+    value_grad = running_kv[1, 0].T.astype(jnp.bfloat16)
     return (query_grad, key_grad, value_grad, weight_grad)
 
 

time: 278 us -> 257 us (0.924)
  waiting for transfers between devices: 173 us -> 153 us
  other arithmetic: 15.2 us -> 4.27 us
  local copies, waits for them, and re-layouts: 22.7 us -> 30.7 us
    ppermute x12, waiting for transfers between devices: 110 us -> 92.9 us  [hop(): return lax.ppermute(slot, 'tensor', ring)]
    unnamed x84 -> x58, local copies, waits for them, and re-layouts: 10.4 us -> 16.9 us
    dot_general x4, matrix products: 9.52 us -> 14.6 us  [weight_term(): lax.dot_general(chunk, attended, (((0,), (0,)), ((), ())), preferred_elem...]
    dot_general x4, matrix products: 14 us -> 9.3 us  [add_term(): term = jnp.dot(chunk, weight, preferred_element_type=jnp.float32)]
    unnamed x3, other arithmetic: 4.02 us -> 0.3 us
    ppermute x12, starting transfers between devices: 4.82 us -> 7.66 us  [hop(): return lax.ppermute(slot, 'tensor', ring)]
  transfers between devices with their start and end apart: 50 -> 50, of which waited for: 19 -> 24; matrix products, arithmetic and copies ran while one was open for 21% -> 21% of each run, Pallas kernels for 4% -> 0%
where the time goes in v1:
time: 257 us; the launch traced here: 256 us
  waiting for transfers between devices  153 us (60%)
  starting transfers between devices  31.4 us (12%)
  local copies, waits for them, and re-layouts  30.7 us (12%)
  matrix products  23.9 us (9%)
  Pallas kernels  11.8 us (5%)
  other arithmetic  4.27 us (2%)
    ppermute x12, waiting for transfers between devices, hop(): return lax.ppermute(slot, 'tensor', ring)  92.9 us
    ppermute x38, waiting for transfers between devices, partner(): return lax.ppermute(value, axis, pairs)  59.7 us
    ppermute x38, starting transfers between devices, partner(): return lax.ppermute(value, axis, pairs)  23.7 us
    unnamed x58, local copies, waits for them, and re-layouts  16.9 us
    dot_general x4, matrix products, weight_term(): lax.dot_general(chunk, attended, (((0,), (0,)), ((), ())), preferred_elem...  14.6 us
    pallas_call x1, Pallas kernels, attention_grads(): pl.pallas_call(functools.partial(attention_kernel, 256), grid=(heads,), i...  11.8 us
    dot_general x4, matrix products, add_term(): term = jnp.dot(chunk, weight, preferred_element_type=jnp.float32)  9.3 us
    ppermute x12, starting transfers between devices, hop(): return lax.ppermute(slot, 'tensor', ring)  7.66 us
  transfers between devices with their start and end apart: 50, of which 24 were waited for; matrix products, arithmetic and copies ran while one was open for 21% of the time, Pallas kernels for 0%

profile of v1, /device:TPU:0, one launch (start us, length us, event | category | flops | bytes accessed | tf_op | source)
XLA Modules:
  0.0 256.3 jit_solution(11397150693987232029)
XLA Ops:
  0.7 3.0 %collective-permute-start.2 = (bf16[2048,512]{1,0:T(8,128)(2,1)}, bf16[2048,512]{1,0:T(8,128)(2,1)}, u32[]{:S(2)}, u32[]{:S(2)}) collective-permute-start(bf16[2048,512]{1,0:T(8,128)(2,1)} %param.8), channel_id=1, source_target_pairs={{0,8},{8,0},{16,24},{24,16},{1,9},{9,1},{17,25},{25,17},{2,10},{10... | collective-permute-start | bytes 6291464 | tf_op jit(solution)/shard_map/ppermute | solution.py:18
  3.7 1.5 collective-permute-start.3
  5.2 2.5 constant_dynamic-slice_fusion.3
  7.7 0.8 pad_maximum_fusion.2
  8.5 1.6 collective-permute-start
  10.2 1.6 collective-permute-start.10
  11.8 1.9 constant_dynamic-update-slice_fusion.15
  15.1 1.0 constant_dynamic-slice_fusion.16
  16.1 0.7 dynamic-slice_dynamic-update-slice_fusion.5
  17.4 0.9 pad_maximum_fusion.4
  18.4 0.7 dynamic-slice_dynamic-update-slice_fusion.3
  19.7 15.3 %collective-permute-done.10 = bf16[128,2048]{1,0:T(8,128)(2,1)} collective-permute-done((bf16[128,2048]{1,0:T(8,128)(2,1)S(1)}, bf16[128,2048]{1,0:T(8,128)(2,1)}, u32[]{:S(2)}, u32[]{:S(2)}) %collective-permute-start.10) | collective-permute-done | bytes 524320 | tf_op jit(solution)/shard_map/ppermute | solution.py:145
  35.7 2.9 %fusion.67 = (bf16[512,512]{1,0:T(8,128)(2,1)}, bf16[512,512]{1,0:T(8,128)(2,1)}, bf16[512,512]{1,0:T(8,128)(2,1)}, bf16[512,512]{1,0:T(8,128)(2,1)}) fusion(bf16[2048,512]{1,0:T(8,128)(2,1)} %param.8), kind=kLoop, calls=%fused_computation.171 | loop fusion | bytes 4194304 | tf_op jit(solution)/shard_map/slice | solution.py:110
  39.5 1.3 collective-permute-start.1
  40.8 11.2 %collective-permute-done.12 = bf16[128,2048]{1,0:T(8,128)(2,1)} collective-permute-done((bf16[128,2048]{1,0:T(8,128)(2,1)}, bf16[128,2048]{1,0:T(8,128)(2,1)}, u32[]{:S(2)}, u32[]{:S(2)}) %collective-permute-start.12) | collective-permute-done | bytes 524320 | tf_op jit(solution)/shard_map/ppermute | solution.py:145
  52.0 1.9 constant_dynamic-update-slice_fusion.14
  53.9 1.9 constant_dynamic-update-slice_fusion.13
  55.7 1.9 constant_dynamic-update-slice_fusion.12
  57.6 14.2 %collective-permute-done.14 = bf16[128,2048]{1,0:T(8,128)(2,1)S(1)} collective-permute-done((bf16[128,2048]{1,0:T(8,128)(2,1)}, bf16[128,2048]{1,0:T(8,128)(2,1)S(1)}, u32[]{:S(2)}, u32[]{:S(2)}) %collective-permute-start.14) | collective-permute-done | bytes 524320 | tf_op jit(solution)/shard_map/ppermute | solution.py:145
  72.6 1.3 slice.270
  74.4 1.3 slice.271
  75.8 0.8 collective-permute-start.8
  76.5 2.8 %fusion.68 = (bf16[512,512]{1,0:T(8,128)(2,1)S(1)}, bf16[512,512]{1,0:T(8,128)(2,1)S(1)}, bf16[512,512]{1,0:T(8,128)(2,1)S(1)}, bf16[512,512]{1,0:T(8,128)(2,1)S...) fusion(bf16[2048,512]{1,0:T(8,128)(2,1)} %collective-permute-do, ...), kind=kLoop, calls=%fused_computation.172 | loop fusion | bytes 8388608 | tf_op jit(solution)/shard_map/slice | solution.py:110
  80.2 7.9 %collective-permute-done.4 = bf16[128,2048]{1,0:T(8,128)(2,1)S(1)} collective-permute-done((bf16[128,2048]{1,0:T(8,128)(2,1)S(1)}, bf16[128,2048]{1,0:T(8,128)(2,1)S(1)}, u32[]{:S(2)}, u32[]{:S(2)}) %collective-permute-start.4) | collective-permute-done | bytes 524320 | tf_op jit(solution)/shard_map/ppermute | solution.py:145
  88.2 10.8 %collective-permute-done.7 = bf16[1024,512]{1,0:T(8,128)(2,1)S(1)} collective-permute-done((bf16[1024,512]{1,0:T(8,128)(2,1)S(1)}, bf16[1024,512]{1,0:T(8,128)(2,1)S(1)}, u32[]{:S(2)}, u32[]{:S(2)}) %collective-permute-start.7) | collective-permute-done | bytes 1048608 | tf_op jit(solution)/shard_map/ppermute | solution.py:18
  99.0 1.6 collective-permute-done.8
  100.8 1.1 constant_dynamic-update-slice_fusion.5
  101.9 1.1 constant_dynamic-update-slice_fusion.3
  103.2 3.6 %convolution_convert_fusion.3 = bf16[2048,512]{1,0:T(8,128)(2,1)S(1)} fusion(bf16[1024,2048]{1,0:T(8,128)(2,1)S(1)} %constant_dynamic-update-slice_fusion, bf16[1024,512]{1,0:T(8,128)(2,1)} %dynamic-slice_dynamic-update-slice_fusion), kind=kOutput, calls=%fused_computation.3 | convolution fusion | flops 2148532224 | bytes 7340032 | tf_op jit(solution)/shard_map/dot_general | solution.py:148
  106.9 1.6 collective-permute-start.22
  109.2 3.7 %convolution_convert_fusion.2 = bf16[2048,512]{1,0:T(8,128)(2,1)S(1)} fusion(bf16[1024,2048]{1,0:T(8,128)(2,1)S(1)} %constant_dynamic-update-slice_fusion.8, bf16[1024,512]{1,0:T(8,128)(2,1)} %dynamic-slice_dynamic-update-slice_fusion), kind=kOutput, calls=%fused_computation.2 | convolution fusion | flops 2148532224 | bytes 7340032 | tf_op jit(solution)/shard_map/dot_general | solution.py:148
  113.0 0.8 collective-permute-start.28
  113.9 1.3 collective-permute-start.30
  115.2 1.9 collective-permute-done.5
  117.1 2.3 fusion.8
  119.4 2.4 collective-permute-done.22
  121.8 1.5 collective-permute-done.24
  124.0 0.7 collective-permute-start.25
  124.8 2.3 fusion.34
  127.1 5.9 %collective-permute-done.28 = bf16[2,256,512]{2,1,0:T(8,128)(2,1)S(1)} collective-permute-done((bf16[2,256,512]{2,1,0:T(8,128)(2,1)S(1)}, bf16[2,256,512]{2,1,0:T(8,128)(2,1)S(1)}, u32[]{:S(2)}, u32[]{:S(2)}) %collective-permute-start.28) | collective-permute-done | bytes 524320 | tf_op jit(solution)/shard_map/ppermute | solution.py:18
  133.0 0.9 collective-permute-start.21
  135.3 4.9 %collective-permute-done.23 = bf16[256,512]{1,0:T(8,128)(2,1)S(1)} collective-permute-done((bf16[256,512]{1,0:T(8,128)(2,1)S(1)}, bf16[256,512]{1,0:T(8,128)(2,1)S(1)}, u32[]{:S(2)}, u32[]{:S(2)}) %collective-permute-start.23) | collective-permute-done | bytes 262176 | tf_op jit(solution)/shard_map/ppermute | solution.py:18
  140.9 7.0 %collective-permute-done.21 = bf16[128,2048]{1,0:T(8,128)(2,1)S(1)} collective-permute-done((bf16[128,2048]{1,0:T(8,128)(2,1)S(1)}, bf16[128,2048]{1,0:T(8,128)(2,1)S(1)}, u32[]{:S(2)}, u32[]{:S(2)}) %collective-permute-start.21) | collective-permute-done | bytes 524320 | tf_op jit(solution)/shard_map/ppermute | solution.py:145
  148.6 2.1 collective-permute-start.38
  151.0 13.6 %collective-permute-done.27 = bf16[128,2048]{1,0:T(8,128)(2,1)S(1)} collective-permute-done((bf16[128,2048]{1,0:T(8,128)(2,1)S(1)}, bf16[128,2048]{1,0:T(8,128)(2,1)S(1)}, u32[]{:S(2)}, u32[]{:S(2)}) %collective-permute-start.27) | collective-permute-done | bytes 524320 | tf_op jit(solution)/shard_map/ppermute | solution.py:145
  164.8 21.8 %collective-permute-done.33 = bf16[128,2048]{1,0:T(8,128)(2,1)S(1)} collective-permute-done((bf16[128,2048]{1,0:T(8,128)(2,1)S(1)}, bf16[128,2048]{1,0:T(8,128)(2,1)S(1)}, u32[]{:S(2)}, u32[]{:S(2)}) %collective-permute-start.33) | collective-permute-done | bytes 524320 | tf_op jit(solution)/shard_map/ppermute | solution.py:145
  187.4 1.1 collective-permute-done.34
  188.6 3.7 %convolution_convert_fusion.1 = bf16[2048,512]{1,0:T(8,128)(2,1)S(1)} fusion(bf16[1024,2048]{1,0:T(8,128)(2,1)S(1)} %constant_dynamic-update-slice_fusion.16, bf16[1024,512]{1,0:T(8,128)(2,1)} %dynamic-slice_dynamic-update-slice_fusion), kind=kOutput, calls=%fused_computation.1 | convolution fusion | flops 2148532224 | bytes 7340032 | tf_op jit(solution)/shard_map/dot_general | solution.py:148
  192.2 2.3 fusion.16
  195.4 1.6 collective-permute-start.40
  197.7 3.7 %convolution_convert_fusion = bf16[2048,512]{1,0:T(8,128)(2,1)S(1)} fusion(bf16[1024,2048]{1,0:T(8,128)(2,1)S(1)} %constant_dynamic-update-slice_fusion.24, bf16[1024,512]{1,0:T(8,128)(2,1)} %dynamic-slice_dynamic-update-slice_fusion), kind=kOutput, calls=%fused_computation | convolution fusion | flops 2148532224 | bytes 7340032 | tf_op jit(solution)/shard_map/dot_general | solution.py:148
  201.4 8.1 %collective-permute-done.40 = bf16[2,256,512]{2,1,0:T(8,128)(2,1)S(1)} collective-permute-done((bf16[2,256,512]{2,1,0:T(8,128)(2,1)S(1)}, bf16[2,256,512]{2,1,0:T(8,128)(2,1)S(1)}, u32[]{:S(2)}, u32[]{:S(2)}) %collective-permute-start.40) | collective-permute-done | bytes 524320 | tf_op jit(solution)/shard_map/ppermute | solution.py:18
  209.5 1.2 collective-permute-done.41
  210.7 2.3 add_convert_fusion
  213.3 11.8 %attention_grads.1 = (bf16[1024,512]{1,0:T(8,128)(2,1)}, f32[128,1024]{1,0:T(8,128)S(1)}, f32[128,1024]{1,0:T(8,128)S(1)}) custom-call(bf16[1024,512]{1,0:T(8,128)(2,1)S(1)} %copy-done.1, bf16[1024,128]{1,0:T(8,128)(2,1)S(1)} %get-tuple-element.123.k_ref, bf16[128,1024]{1,0:T(8,128)(2,1)S(1)} %bitcast.101, bf16[1024,128]{1,0:T(8,128)(2,1)S(1)} %get-tuple-element.122.v_ref, ...), custom_call_target="tpu_custom_call" | custom-call | flops 5368709120 | bytes 5242880 | tf_op jit(solution)/shard_map/attention_grads/pallas_call | solution.py:72
  226.1 0.7 collective-permute-start.45
  226.9 1.4 collective-permute-start.48
  228.3 1.6 collective-permute-start.46
  230.1 4.6 %collective-permute-done.44 = bf16[256,512]{1,0:T(8,128)(2,1)S(1)} collective-permute-done((bf16[256,512]{1,0:T(8,128)(2,1)S(1)}, bf16[256,512]{1,0:T(8,128)(2,1)S(1)}, u32[]{:S(2)}, u32[]{:S(2)}) %collective-permute-start.44) | collective-permute-done | bytes 262176 | tf_op jit(solution)/shard_map/ppermute | solution.py:18
  235.4 10.1 %collective-permute-done.48 = bf16[2,256,512]{2,1,0:T(8,128)(2,1)S(1)} collective-permute-done((bf16[2,256,512]{2,1,0:T(8,128)(2,1)S(1)}, bf16[2,256,512]{2,1,0:T(8,128)(2,1)S(1)}, u32[]{:S(2)}, u32[]{:S(2)}) %collective-permute-start.48) | collective-permute-done | bytes 524320 | tf_op jit(solution)/shard_map/ppermute | solution.py:18
  245.9 1.6 collective-permute-start.47
  248.8 4.8 %collective-permute-done.47 = bf16[256,512]{1,0:T(8,128)(2,1)S(1)} collective-permute-done((bf16[256,512]{1,0:T(8,128)(2,1)S(1)}, bf16[256,512]{1,0:T(8,128)(2,1)S(1)}, u32[]{:S(2)}, u32[]{:S(2)}) %collective-permute-start.47) | collective-permute-done | bytes 262176 | tf_op jit(solution)/shard_map/ppermute | solution.py:18
  253.7 1.2 collective-permute-done.49
  255.0 1.3 copy-done.7
  (160 shorter events, 17.6 us)
Async XLA Ops:
  0.6 13.1 %copy-start = (bf16[1024,512]{1,0:T(8,128)(2,1)S(1)}, bf16[1024,512]{1,0:T(8,128)(2,1)}, u32[]{:S(2)}) copy-start(bf16[1024,512]{1,0:T(8,128)(2,1)} %o_ref.1) | copy-start | bytes 3145732
  0.6 14.4 %copy-start.8 = (bf16[1024,256]{1,0:T(8,128)(2,1)S(1)}, bf16[1024,256]{1,0:T(8,128)(2,1)}, u32[]{:S(2)}) copy-start(bf16[1024,256]{1,0:T(8,128)(2,1)} %param.11) | copy-start | bytes 1572868
  0.7 71.2 %collective-permute-start.2 = (bf16[2048,512]{1,0:T(8,128)(2,1)}, bf16[2048,512]{1,0:T(8,128)(2,1)}, u32[]{:S(2)}, u32[]{:S(2)}) collective-permute-start(bf16[2048,512]{1,0:T(8,128)(2,1)} %param.8), channel_id=1, source_target_pairs={{0,8},{8,0},{16,24},{24,16},{1,9},{9,1},{17,25},{25,17},{2,10},{10... | collective-permute-start | bytes 6291464 | tf_op jit(solution)/shard_map/ppermute | solution.py:18
  3.7 68.2 %collective-permute-start.3 = (bf16[2048,512]{1,0:T(8,128)(2,1)}, bf16[2048,512]{1,0:T(8,128)(2,1)}, u32[]{:S(2)}, u32[]{:S(2)}) collective-permute-start(bf16[2048,512]{1,0:T(8,128)(2,1)} %param.8), channel_id=1, source_target_pairs={{0,16},{8,24},{16,0},{24,8},{1,17},{9,25},{17,1},{25,9},{2,18},{10... | collective-permute-start | bytes 6291464 | tf_op jit(solution)/shard_map/ppermute | solution.py:18
  8.5 30.1 %collective-permute-start = (bf16[128,2048]{1,0:T(8,128)(2,1)}, bf16[128,2048]{1,0:T(8,128)(2,1)}, u32[]{:S(2)}, u32[]{:S(2)}) collective-permute-start(bf16[128,2048]{1,0:T(8,128)(2,1)} %pad_maximum_fusion.2), channel_id=1, source_target_pairs={{0,2},{1,3},{2,4},{3,5},{4,6},{5,7},{6,0},{7,1},{8,10},{9,11},{10,... | collective-permute-start | bytes 1572872 | tf_op jit(solution)/shard_map/ppermute | solution.py:145
  10.1 29.3 %collective-permute-start.16 = (bf16[128,2048]{1,0:T(8,128)(2,1)}, bf16[128,2048]{1,0:T(8,128)(2,1)}, u32[]{:S(2)}, u32[]{:S(2)}) collective-permute-start(bf16[128,2048]{1,0:T(8,128)(2,1)} %pad_maximum_fusion.2), channel_id=1, source_target_pairs={{0,1},{1,0},{2,3},{3,2},{4,5},{5,4},{6,7},{7,6},{8,9},{9,8},{10,11... | collective-permute-start | bytes 1572872 | tf_op jit(solution)/shard_map/ppermute | solution.py:18
  10.2 24.9 %collective-permute-start.10 = (bf16[128,2048]{1,0:T(8,128)(2,1)S(1)}, bf16[128,2048]{1,0:T(8,128)(2,1)}, u32[]{:S(2)}, u32[]{:S(2)}) collective-permute-start(bf16[128,2048]{1,0:T(8,128)(2,1)S(1)} %pad_maximum_fusion.3), channel_id=1, source_target_pairs={{0,2},{1,3},{2,4},{3,5},{4,6},{5,7},{6,0},{7,1},{8,10},{9,11},{10,... | collective-permute-start | bytes 1572872 | tf_op jit(solution)/shard_map/ppermute | solution.py:145
  35.1 16.9 %collective-permute-start.12 = (bf16[128,2048]{1,0:T(8,128)(2,1)}, bf16[128,2048]{1,0:T(8,128)(2,1)}, u32[]{:S(2)}, u32[]{:S(2)}) collective-permute-start(bf16[128,2048]{1,0:T(8,128)(2,1)} %collective-permute-done.10), channel_id=1, source_target_pairs={{0,2},{1,3},{2,4},{3,5},{4,6},{5,7},{6,0},{7,1},{8,10},{9,11},{10,... | collective-permute-start | bytes 1572872 | tf_op jit(solution)/shard_map/ppermute | solution.py:145
  38.6 17.1 %collective-permute-start.17 = (bf16[128,2048]{1,0:T(8,128)(2,1)}, bf16[128,2048]{1,0:T(8,128)(2,1)}, u32[]{:S(2)}, u32[]{:S(2)}) collective-permute-start(bf16[128,2048]{1,0:T(8,128)(2,1)} %collective-permute-done), channel_id=1, source_target_pairs={{0,1},{1,0},{2,3},{3,2},{4,5},{5,4},{6,7},{7,6},{8,9},{9,8},{10,11... | collective-permute-start | bytes 1572872 | tf_op jit(solution)/shard_map/ppermute | solution.py:18
  39.5 32.4 %collective-permute-start.1 = (bf16[128,2048]{1,0:T(8,128)(2,1)}, bf16[128,2048]{1,0:T(8,128)(2,1)S(1)}, u32[]{:S(2)}, u32[]{:S(2)}) collective-permute-start(bf16[128,2048]{1,0:T(8,128)(2,1)} %collective-permute-done), channel_id=1, source_target_pairs={{0,2},{1,3},{2,4},{3,5},{4,6},{5,7},{6,0},{7,1},{8,10},{9,11},{10,... | collective-permute-start | bytes 1572872 | tf_op jit(solution)/shard_map/ppermute | solution.py:145
  52.0 19.9 %collective-permute-start.14 = (bf16[128,2048]{1,0:T(8,128)(2,1)}, bf16[128,2048]{1,0:T(8,128)(2,1)S(1)}, u32[]{:S(2)}, u32[]{:S(2)}) collective-permute-start(bf16[128,2048]{1,0:T(8,128)(2,1)} %collective-permute-done.12), channel_id=1, source_target_pairs={{0,2},{1,3},{2,4},{3,5},{4,6},{5,7},{6,0},{7,1},{8,10},{9,11},{10,... | collective-permute-start | bytes 1572872 | tf_op jit(solution)/shard_map/ppermute | solution.py:145
  71.8 7.6 %collective-permute-start.20 = (bf16[128,2048]{1,0:T(8,128)(2,1)S(1)}, bf16[128,2048]{1,0:T(8,128)(2,1)S(1)}, u32[]{:S(2)}, u32[]{:S(2)}) collective-permute-start(bf16[128,2048]{1,0:T(8,128)(2,1)S(1)} %pad_maximum_fusion.4), channel_id=1, source_target_pairs={{0,1},{1,0},{2,3},{3,2},{4,5},{5,4},{6,7},{7,6},{8,9},{9,8},{10,11... | collective-permute-start | bytes 1572872 | tf_op jit(solution)/shard_map/ppermute | solution.py:18
  71.9 16.2 %collective-permute-start.4 = (bf16[128,2048]{1,0:T(8,128)(2,1)S(1)}, bf16[128,2048]{1,0:T(8,128)(2,1)S(1)}, u32[]{:S(2)}, u32[]{:S(2)}) collective-permute-start(bf16[128,2048]{1,0:T(8,128)(2,1)S(1)} %collective-permute-done.1), channel_id=1, source_target_pairs={{0,2},{1,3},{2,4},{3,5},{4,6},{5,7},{6,0},{7,1},{8,10},{9,11},{10,... | collective-permute-start | bytes 1572872 | tf_op jit(solution)/shard_map/ppermute | solution.py:145
  72.0 7.6 %collective-permute-start.18 = (bf16[128,2048]{1,0:T(8,128)(2,1)S(1)}, bf16[128,2048]{1,0:T(8,128)(2,1)S(1)}, u32[]{:S(2)}, u32[]{:S(2)}) collective-permute-start(bf16[128,2048]{1,0:T(8,128)(2,1)S(1)} %collective-permute-done.1), channel_id=1, source_target_pairs={{0,1},{1,0},{2,3},{3,2},{4,5},{5,4},{6,7},{7,6},{8,9},{9,8},{10,11... | collective-permute-start | bytes 1572872 | tf_op jit(solution)/shard_map/ppermute | solution.py:18
  73.8 25.1 %collective-permute-start.7 = (bf16[1024,512]{1,0:T(8,128)(2,1)S(1)}, bf16[1024,512]{1,0:T(8,128)(2,1)S(1)}, u32[]{:S(2)}, u32[]{:S(2)}) collective-permute-start(bf16[1024,512]{1,0:T(8,128)(2,1)S(1)} %slice.270), channel_id=1, source_target_pairs={{0,8},{8,0},{16,24},{24,16},{1,9},{9,1},{17,25},{25,17},{2,10},{10... | collective-permute-start | bytes 3145736 | tf_op jit(solution)/shard_map/ppermute | solution.py:18
  75.7 3.6 %copy-start.9 = (bf16[1024,2048]{1,0:T(8,128)(2,1)S(1)}, bf16[1024,2048]{1,0:T(8,128)(2,1)}, u32[]{:S(2)}) copy-start(bf16[1024,2048]{1,0:T(8,128)(2,1)} %constant_dynamic-update-slice_fusion.12) | copy-start | bytes 12582916
  75.8 24.9 %collective-permute-start.8 = (bf16[1024,512]{1,0:T(8,128)(2,1)S(1)}, bf16[1024,512]{1,0:T(8,128)(2,1)S(1)}, u32[]{:S(2)}, u32[]{:S(2)}) collective-permute-start(bf16[1024,512]{1,0:T(8,128)(2,1)S(1)} %slice.271), channel_id=1, source_target_pairs={{0,16},{8,24},{16,0},{24,8},{1,17},{9,25},{17,1},{25,9},{2,18},{10... | collective-permute-start | bytes 3145736 | tf_op jit(solution)/shard_map/ppermute | solution.py:18
  79.4 21.2 %collective-permute-start.9 = (bf16[128,2048]{1,0:T(8,128)(2,1)S(1)}, bf16[128,2048]{1,0:T(8,128)(2,1)S(1)}, u32[]{:S(2)}, u32[]{:S(2)}) collective-permute-start(bf16[128,2048]{1,0:T(8,128)(2,1)S(1)} %pad_maximum_fusion.3), channel_id=1, source_target_pairs={{0,1},{1,0},{2,3},{3,2},{4,5},{5,4},{6,7},{7,6},{8,9},{9,8},{10,11... | collective-permute-start | bytes 1572872 | tf_op jit(solution)/shard_map/ppermute | solution.py:18
  79.6 22.3 %collective-permute-start.11 = (bf16[128,2048]{1,0:T(8,128)(2,1)}, bf16[128,2048]{1,0:T(8,128)(2,1)S(1)}, u32[]{:S(2)}, u32[]{:S(2)}) collective-permute-start(bf16[128,2048]{1,0:T(8,128)(2,1)} %collective-permute-done.10), channel_id=1, source_target_pairs={{0,1},{1,0},{2,3},{3,2},{4,5},{5,4},{6,7},{7,6},{8,9},{9,8},{10,11... | collective-permute-start | bytes 1572872 | tf_op jit(solution)/shard_map/ppermute | solution.py:18
  88.1 14.9 %collective-permute-start.13 = (bf16[128,2048]{1,0:T(8,128)(2,1)}, bf16[128,2048]{1,0:T(8,128)(2,1)S(1)}, u32[]{:S(2)}, u32[]{:S(2)}) collective-permute-start(bf16[128,2048]{1,0:T(8,128)(2,1)} %collective-permute-done.12), channel_id=1, source_target_pairs={{0,1},{1,0},{2,3},{3,2},{4,5},{5,4},{6,7},{7,6},{8,9},{9,8},{10,11... | collective-permute-start | bytes 1572872 | tf_op jit(solution)/shard_map/ppermute | solution.py:18
  99.0 4.1 %collective-permute-start.15 = (bf16[128,2048]{1,0:T(8,128)(2,1)S(1)}, bf16[128,2048]{1,0:T(8,128)(2,1)S(1)}, u32[]{:S(2)}, u32[]{:S(2)}) collective-permute-start(bf16[128,2048]{1,0:T(8,128)(2,1)S(1)} %collective-permute-done.14), channel_id=1, source_target_pairs={{0,1},{1,0},{2,3},{3,2},{4,5},{5,4},{6,7},{7,6},{8,9},{9,8},{10,11... | collective-permute-start | bytes 1572872 | tf_op jit(solution)/shard_map/ppermute | solution.py:18
  100.6 8.5 %collective-permute-start.19 = (bf16[128,2048]{1,0:T(8,128)(2,1)S(1)}, bf16[128,2048]{1,0:T(8,128)(2,1)S(1)}, u32[]{:S(2)}, u32[]{:S(2)}) collective-permute-start(bf16[128,2048]{1,0:T(8,128)(2,1)S(1)} %collective-permute-done.4), channel_id=1, source_target_pairs={{0,1},{1,0},{2,3},{3,2},{4,5},{5,4},{6,7},{7,6},{8,9},{9,8},{10,11... | collective-permute-start | bytes 1572872 | tf_op jit(solution)/shard_map/ppermute | solution.py:18
  100.7 16.4 %collective-permute-start.5 = (bf16[128,2048]{1,0:T(8,128)(2,1)S(1)}, bf16[128,2048]{1,0:T(8,128)(2,1)S(1)}, u32[]{:S(2)}, u32[]{:S(2)}) collective-permute-start(bf16[128,2048]{1,0:T(8,128)(2,1)S(1)} %pad_maximum_fusion.1), channel_id=1, source_target_pairs={{0,2},{1,3},{2,4},{3,5},{4,6},{5,7},{6,0},{7,1},{8,10},{9,11},{10,... | collective-permute-start | bytes 1572872 | tf_op jit(solution)/shard_map/ppermute | solution.py:145
  106.9 14.9 %collective-permute-start.22 = (bf16[2,256,512]{2,1,0:T(8,128)(2,1)S(1)}, bf16[2,256,512]{2,1,0:T(8,128)(2,1)S(1)}, u32[]{:S(2)}, u32[]{:S(2)}) collective-permute-start(bf16[2,256,512]{2,1,0:T(8,128)(2,1)S(1)} %pad_maximum_fusion.5), channel_id=1, source_target_pairs={{0,8},{8,0},{16,24},{24,16},{1,9},{9,1},{17,25},{25,17},{2,10},{10... | collective-permute-start | bytes 1572872 | tf_op jit(solution)/shard_map/ppermute | solution.py:18
  108.5 14.8 %collective-permute-start.24 = (bf16[2,256,512]{2,1,0:T(8,128)(2,1)S(1)}, bf16[2,256,512]{2,1,0:T(8,128)(2,1)S(1)}, u32[]{:S(2)}, u32[]{:S(2)}) collective-permute-start(bf16[2,256,512]{2,1,0:T(8,128)(2,1)S(1)} %slice.353), channel_id=1, source_target_pairs={{0,16},{8,24},{16,0},{24,8},{1,17},{9,25},{17,1},{25,9},{2,18},{10... | collective-permute-start | bytes 1572872 | tf_op jit(solution)/shard_map/ppermute | solution.py:18
  109.2 7.8 %copy-start.6 = (bf16[512,512]{1,0:T(8,128)(2,1)S(1)}, bf16[512,512]{1,0:T(8,128)(2,1)}, u32[]{:S(2)}) copy-start(bf16[512,512]{1,0:T(8,128)(2,1)} %get-tuple-element.73) | copy-start | bytes 1572868
  113.0 20.0 %collective-permute-start.28 = (bf16[2,256,512]{2,1,0:T(8,128)(2,1)S(1)}, bf16[2,256,512]{2,1,0:T(8,128)(2,1)S(1)}, u32[]{:S(2)}, u32[]{:S(2)}) collective-permute-start(bf16[2,256,512]{2,1,0:T(8,128)(2,1)S(1)} %pad_maximum_fusion.7), channel_id=1, source_target_pairs={{0,8},{8,0},{16,24},{24,16},{1,9},{9,1},{17,25},{25,17},{2,10},{10... | collective-permute-start | bytes 1572872 | tf_op jit(solution)/shard_map/ppermute | solution.py:18
  113.9 20.7 %collective-permute-start.30 = (bf16[2,256,512]{2,1,0:T(8,128)(2,1)S(1)}, bf16[2,256,512]{2,1,0:T(8,128)(2,1)S(1)}, u32[]{:S(2)}, u32[]{:S(2)}) collective-permute-start(bf16[2,256,512]{2,1,0:T(8,128)(2,1)S(1)} %slice.364), channel_id=1, source_target_pairs={{0,16},{8,24},{16,0},{24,8},{1,17},{9,25},{17,1},{25,9},{2,18},{10... | collective-permute-start | bytes 1572872 | tf_op jit(solution)/shard_map/ppermute | solution.py:18
  117.1 17.6 %collective-permute-start.6 = (bf16[128,2048]{1,0:T(8,128)(2,1)S(1)}, bf16[128,2048]{1,0:T(8,128)(2,1)S(1)}, u32[]{:S(2)}, u32[]{:S(2)}) collective-permute-start(bf16[128,2048]{1,0:T(8,128)(2,1)S(1)} %collective-permute-done.5), channel_id=1, source_target_pairs={{0,2},{1,3},{2,4},{3,5},{4,6},{5,7},{6,0},{7,1},{8,10},{9,11},{10,... | collective-permute-start | bytes 1572872 | tf_op jit(solution)/shard_map/ppermute | solution.py:145
  117.1 7.7 %copy-start.5 = (bf16[512,512]{1,0:T(8,128)(2,1)S(1)}, bf16[512,512]{1,0:T(8,128)(2,1)}, u32[]{:S(2)}) copy-start(bf16[512,512]{1,0:T(8,128)(2,1)} %get-tuple-element.74) | copy-start | bytes 1572868
  123.4 16.7 %collective-permute-start.23 = (bf16[256,512]{1,0:T(8,128)(2,1)S(1)}, bf16[256,512]{1,0:T(8,128)(2,1)S(1)}, u32[]{:S(2)}, u32[]{:S(2)}) collective-permute-start(bf16[256,512]{1,0:T(8,128)(2,1)S(1)} %get-tuple-element.94), channel_id=1, source_target_pairs={{0,16},{8,24},{16,0},{24,8},{1,17},{9,25},{17,1},{25,9},{2,18},{10... | collective-permute-start | bytes 786440 | tf_op jit(solution)/shard_map/ppermute | solution.py:18
  124.0 16.7 %collective-permute-start.25 = (bf16[256,512]{1,0:T(8,128)(2,1)S(1)}, bf16[256,512]{1,0:T(8,128)(2,1)S(1)}, u32[]{:S(2)}, u32[]{:S(2)}) collective-permute-start(bf16[256,512]{1,0:T(8,128)(2,1)S(1)} %get-tuple-element.95), channel_id=1, source_target_pairs={{0,8},{8,0},{16,24},{24,16},{1,9},{9,1},{17,25},{25,17},{2,10},{10... | collective-permute-start | bytes 786440 | tf_op jit(solution)/shard_map/ppermute | solution.py:18
  133.0 14.9 %collective-permute-start.21 = (bf16[128,2048]{1,0:T(8,128)(2,1)S(1)}, bf16[128,2048]{1,0:T(8,128)(2,1)S(1)}, u32[]{:S(2)}, u32[]{:S(2)}) collective-permute-start(bf16[128,2048]{1,0:T(8,128)(2,1)S(1)} %pad_maximum_fusion.4), channel_id=1, source_target_pairs={{0,2},{1,3},{2,4},{3,5},{4,6},{5,7},{6,0},{7,1},{8,10},{9,11},{10,... | collective-permute-start | bytes 1572872 | tf_op jit(solution)/shard_map/ppermute | solution.py:145
  134.5 60.6 %collective-permute-start.35 = (bf16[128,2048]{1,0:T(8,128)(2,1)S(1)}, bf16[128,2048]{1,0:T(8,128)(2,1)S(1)}, u32[]{:S(2)}, u32[]{:S(2)}) collective-permute-start(bf16[128,2048]{1,0:T(8,128)(2,1)S(1)} %pad_maximum_fusion.1), channel_id=1, source_target_pairs={{0,1},{1,0},{2,3},{3,2},{4,5},{5,4},{6,7},{7,6},{8,9},{9,8},{10,11... | collective-permute-start | bytes 1572872 | tf_op jit(solution)/shard_map/ppermute | solution.py:18
  134.7 13.4 %collective-permute-start.29 = (bf16[256,512]{1,0:T(8,128)(2,1)S(1)}, bf16[256,512]{1,0:T(8,128)(2,1)S(1)}, u32[]{:S(2)}, u32[]{:S(2)}) collective-permute-start(bf16[256,512]{1,0:T(8,128)(2,1)S(1)} %get-tuple-element.88), channel_id=1, source_target_pairs={{0,16},{8,24},{16,0},{24,8},{1,17},{9,25},{17,1},{25,9},{2,18},{10... | collective-permute-start | bytes 786440 | tf_op jit(solution)/shard_map/ppermute | solution.py:18
  140.2 8.5 %collective-permute-start.31 = (bf16[256,512]{1,0:T(8,128)(2,1)S(1)}, bf16[256,512]{1,0:T(8,128)(2,1)S(1)}, u32[]{:S(2)}, u32[]{:S(2)}) collective-permute-start(bf16[256,512]{1,0:T(8,128)(2,1)S(1)} %get-tuple-element.89), channel_id=1, source_target_pairs={{0,8},{8,0},{16,24},{24,16},{1,9},{9,1},{17,25},{25,17},{2,10},{10... | collective-permute-start | bytes 786440 | tf_op jit(solution)/shard_map/ppermute | solution.py:18
  148.0 16.6 %collective-permute-start.26 = (bf16[128,2048]{1,0:T(8,128)(2,1)S(1)}, bf16[128,2048]{1,0:T(8,128)(2,1)S(1)}, u32[]{:S(2)}, u32[]{:S(2)}) collective-permute-start(bf16[128,2048]{1,0:T(8,128)(2,1)S(1)} %collective-permute-done.21), channel_id=1, source_target_pairs={{0,1},{1,0},{2,3},{3,2},{4,5},{5,4},{6,7},{7,6},{8,9},{9,8},{10,11... | collective-permute-start | bytes 1572872 | tf_op jit(solution)/shard_map/ppermute | solution.py:18
  148.0 16.6 %collective-permute-start.27 = (bf16[128,2048]{1,0:T(8,128)(2,1)S(1)}, bf16[128,2048]{1,0:T(8,128)(2,1)S(1)}, u32[]{:S(2)}, u32[]{:S(2)}) collective-permute-start(bf16[128,2048]{1,0:T(8,128)(2,1)S(1)} %collective-permute-done.21), channel_id=1, source_target_pairs={{0,2},{1,3},{2,4},{3,5},{4,6},{5,7},{6,0},{7,1},{8,10},{9,11},{10,... | collective-permute-start | bytes 1572872 | tf_op jit(solution)/shard_map/ppermute | solution.py:145
  148.1 47.1 %collective-permute-start.36 = (bf16[128,2048]{1,0:T(8,128)(2,1)S(1)}, bf16[128,2048]{1,0:T(8,128)(2,1)S(1)}, u32[]{:S(2)}, u32[]{:S(2)}) collective-permute-start(bf16[128,2048]{1,0:T(8,128)(2,1)S(1)} %collective-permute-done.5), channel_id=1, source_target_pairs={{0,1},{1,0},{2,3},{3,2},{4,5},{5,4},{6,7},{7,6},{8,9},{9,8},{10,11... | collective-permute-start | bytes 1572872 | tf_op jit(solution)/shard_map/ppermute | solution.py:18
  148.6 38.0 %collective-permute-start.38 = (bf16[128,2048]{1,0:T(8,128)(2,1)S(1)}, bf16[128,2048]{1,0:T(8,128)(2,1)S(1)}, u32[]{:S(2)}, u32[]{:S(2)}) collective-permute-start(bf16[128,2048]{1,0:T(8,128)(2,1)S(1)} %collective-permute-done.6), channel_id=1, source_target_pairs={{0,2},{1,3},{2,4},{3,5},{4,6},{5,7},{6,0},{7,1},{8,10},{9,11},{10,... | collective-permute-start | bytes 1572872 | tf_op jit(solution)/shard_map/ppermute | solution.py:145
  164.6 22.0 %collective-permute-start.33 = (bf16[128,2048]{1,0:T(8,128)(2,1)S(1)}, bf16[128,2048]{1,0:T(8,128)(2,1)S(1)}, u32[]{:S(2)}, u32[]{:S(2)}) collective-permute-start(bf16[128,2048]{1,0:T(8,128)(2,1)S(1)} %collective-permute-done.27), channel_id=1, source_target_pairs={{0,2},{1,3},{2,4},{3,5},{4,6},{5,7},{6,0},{7,1},{8,10},{9,11},{10,... | collective-permute-start | bytes 1572872 | tf_op jit(solution)/shard_map/ppermute | solution.py:145
  164.6 22.6 %collective-permute-start.32 = (bf16[128,2048]{1,0:T(8,128)(2,1)S(1)}, bf16[128,2048]{1,0:T(8,128)(2,1)S(1)}, u32[]{:S(2)}, u32[]{:S(2)}) collective-permute-start(bf16[128,2048]{1,0:T(8,128)(2,1)S(1)} %collective-permute-done.27), channel_id=1, source_target_pairs={{0,1},{1,0},{2,3},{3,2},{4,5},{5,4},{6,7},{7,6},{8,9},{9,8},{10,11... | collective-permute-start | bytes 1572872 | tf_op jit(solution)/shard_map/ppermute | solution.py:18
  186.6 1.9 collective-permute-start.34
  186.6 10.9 %collective-permute-start.37 = (bf16[128,2048]{1,0:T(8,128)(2,1)S(1)}, bf16[128,2048]{1,0:T(8,128)(2,1)S(1)}, u32[]{:S(2)}, u32[]{:S(2)}) collective-permute-start(bf16[128,2048]{1,0:T(8,128)(2,1)S(1)} %collective-permute-done.6), channel_id=1, source_target_pairs={{0,1},{1,0},{2,3},{3,2},{4,5},{5,4},{6,7},{7,6},{8,9},{9,8},{10,11... | collective-permute-start | bytes 1572872 | tf_op jit(solution)/shard_map/ppermute | solution.py:18
  187.2 10.4 %collective-permute-start.39 = (bf16[128,2048]{1,0:T(8,128)(2,1)S(1)}, bf16[128,2048]{1,0:T(8,128)(2,1)S(1)}, u32[]{:S(2)}, u32[]{:S(2)}) collective-permute-start(bf16[128,2048]{1,0:T(8,128)(2,1)S(1)} %collective-permute-done.38), channel_id=1, source_target_pairs={{0,1},{1,0},{2,3},{3,2},{4,5},{5,4},{6,7},{7,6},{8,9},{9,8},{10,11... | collective-permute-start | bytes 1572872 | tf_op jit(solution)/shard_map/ppermute | solution.py:18
  188.5 3.7 %copy-start.4 = (bf16[512,512]{1,0:T(8,128)(2,1)S(1)}, bf16[512,512]{1,0:T(8,128)(2,1)}, u32[]{:S(2)}) copy-start(bf16[512,512]{1,0:T(8,128)(2,1)} %get-tuple-element.75) | copy-start | bytes 1572868
  195.4 14.0 %collective-permute-start.40 = (bf16[2,256,512]{2,1,0:T(8,128)(2,1)S(1)}, bf16[2,256,512]{2,1,0:T(8,128)(2,1)S(1)}, u32[]{:S(2)}, u32[]{:S(2)}) collective-permute-start(bf16[2,256,512]{2,1,0:T(8,128)(2,1)S(1)} %pad_maximum_fusion.9), channel_id=1, source_target_pairs={{0,8},{8,0},{16,24},{24,16},{1,9},{9,1},{17,25},{25,17},{2,10},{10... | collective-permute-start | bytes 1572872 | tf_op jit(solution)/shard_map/ppermute | solution.py:18
  197.0 13.7 %collective-permute-start.41 = (bf16[2,256,512]{2,1,0:T(8,128)(2,1)S(1)}, bf16[2,256,512]{2,1,0:T(8,128)(2,1)S(1)}, u32[]{:S(2)}, u32[]{:S(2)}) collective-permute-start(bf16[2,256,512]{2,1,0:T(8,128)(2,1)S(1)} %slice.370), channel_id=1, source_target_pairs={{0,16},{8,24},{16,0},{24,8},{1,17},{9,25},{17,1},{25,9},{2,18},{10... | collective-permute-start | bytes 1572872 | tf_op jit(solution)/shard_map/ppermute | solution.py:18
  197.7 13.0 %copy-start.3 = (bf16[512,512]{1,0:T(8,128)(2,1)S(1)}, bf16[512,512]{1,0:T(8,128)(2,1)}, u32[]{:S(2)}) copy-start(bf16[512,512]{1,0:T(8,128)(2,1)} %get-tuple-element.72) | copy-start | bytes 1572868
  210.7 2.6 %copy-start.1 = (bf16[1024,512]{1,0:T(8,128)(2,1)S(1)}, bf16[1024,512]{1,0:T(8,128)(2,1)}, u32[]{:S(2)}) copy-start(bf16[1024,512]{1,0:T(8,128)(2,1)} %q_ref.1) | copy-start | bytes 3145732
  210.7 2.6 %copy-start.2 = (f32[4,1024]{1,0:T(4,128)S(1)}, f32[4,1024]{1,0:T(4,128)}, u32[]{:S(2)}) copy-start(f32[4,1024]{1,0:T(4,128)} %s_ref.1) | copy-start | bytes 49156
  225.3 4.6 %collective-permute-start.42 = (bf16[2,2,32,1024]{3,2,0,1:T(8,128)(2,1)S(1)}, bf16[2,2,32,1024]{3,2,0,1:T(8,128)(2,1)S(1)}, u32[]{:S(2)}, u32[]{:S(2)}) collective-permute-start(bf16[2,2,32,1024]{3,2,0,1:T(8,128)(2,1)S(1)} %fusion.51), channel_id=1, source_target_pairs={{0,1},{1,0},{2,3},{3,2},{4,5},{5,4},{6,7},{7,6},{8,9},{9,8},{10,11... | collective-permute-start | bytes 786440 | tf_op jit(solution)/shard_map/ppermute | solution.py:18
  225.5 9.2 %collective-permute-start.44 = (bf16[256,512]{1,0:T(8,128)(2,1)S(1)}, bf16[256,512]{1,0:T(8,128)(2,1)S(1)}, u32[]{:S(2)}, u32[]{:S(2)}) collective-permute-start(bf16[256,512]{1,0:T(8,128)(2,1)S(1)} %get-tuple-element.71), channel_id=1, source_target_pairs={{0,16},{8,24},{16,0},{24,8},{1,17},{9,25},{17,1},{25,9},{2,18},{10... | collective-permute-start | bytes 786440 | tf_op jit(solution)/shard_map/ppermute | solution.py:18
  226.1 9.2 %collective-permute-start.45 = (bf16[256,512]{1,0:T(8,128)(2,1)S(1)}, bf16[256,512]{1,0:T(8,128)(2,1)S(1)}, u32[]{:S(2)}, u32[]{:S(2)}) collective-permute-start(bf16[256,512]{1,0:T(8,128)(2,1)S(1)} %get-tuple-element.70), channel_id=1, source_target_pairs={{0,8},{8,0},{16,24},{24,16},{1,9},{9,1},{17,25},{25,17},{2,10},{10... | collective-permute-start | bytes 786440 | tf_op jit(solution)/shard_map/ppermute | solution.py:18
  226.9 18.6 %collective-permute-start.48 = (bf16[2,256,512]{2,1,0:T(8,128)(2,1)S(1)}, bf16[2,256,512]{2,1,0:T(8,128)(2,1)S(1)}, u32[]{:S(2)}, u32[]{:S(2)}) collective-permute-start(bf16[2,256,512]{2,1,0:T(8,128)(2,1)S(1)} %slice.396), channel_id=1, source_target_pairs={{0,16},{8,24},{16,0},{24,8},{1,17},{9,25},{17,1},{25,9},{2,18},{10... | collective-permute-start | bytes 1572872 | tf_op jit(solution)/shard_map/ppermute | solution.py:18
  228.3 17.4 %collective-permute-start.46 = (bf16[2,256,512]{2,1,0:T(8,128)(2,1)S(1)}, bf16[2,256,512]{2,1,0:T(8,128)(2,1)S(1)}, u32[]{:S(2)}, u32[]{:S(2)}) collective-permute-start(bf16[2,256,512]{2,1,0:T(8,128)(2,1)S(1)} %pad_maximum_fusion.10), channel_id=1, source_target_pairs={{0,8},{8,0},{16,24},{24,16},{1,9},{9,1},{17,25},{25,17},{2,10},{10... | collective-permute-start | bytes 1572872 | tf_op jit(solution)/shard_map/ppermute | solution.py:18
  230.0 17.4 %collective-permute-start.43 = (bf16[2,1,32,1024]{3,2,1,0:T(8,128)(2,1)S(1)}, bf16[2,1,32,1024]{3,2,1,0:T(8,128)(2,1)S(1)}, u32[]{:S(2)}, u32[]{:S(2)}) collective-permute-start(bf16[2,1,32,1024]{3,2,1,0:T(8,128)(2,1)S(1)} %fusion.61), channel_id=1, source_target_pairs={{0,2},{1,3},{2,0},{3,1},{4,6},{5,7},{6,4},{7,5},{8,10},{9,11},{10,... | collective-permute-start | bytes 393224 | tf_op jit(solution)/shard_map/ppermute | solution.py:18
  245.9 7.7 %collective-permute-start.47 = (bf16[256,512]{1,0:T(8,128)(2,1)S(1)}, bf16[256,512]{1,0:T(8,128)(2,1)S(1)}, u32[]{:S(2)}, u32[]{:S(2)}) collective-permute-start(bf16[256,512]{1,0:T(8,128)(2,1)S(1)} %get-tuple-element.67), channel_id=1, source_target_pairs={{0,16},{8,24},{16,0},{24,8},{1,17},{9,25},{17,1},{25,9},{2,18},{10... | collective-permute-start | bytes 786440 | tf_op jit(solution)/shard_map/ppermute | solution.py:18
  247.5 7.3 %collective-permute-start.49 = (bf16[256,512]{1,0:T(8,128)(2,1)S(1)}, bf16[256,512]{1,0:T(8,128)(2,1)S(1)}, u32[]{:S(2)}, u32[]{:S(2)}) collective-permute-start(bf16[256,512]{1,0:T(8,128)(2,1)S(1)} %get-tuple-element.66), channel_id=1, source_target_pairs={{0,8},{8,0},{16,24},{24,16},{1,9},{9,1},{17,25},{25,17},{2,10},{10... | collective-permute-start | bytes 786440 | tf_op jit(solution)/shard_map/ppermute | solution.py:18
  255.0 1.3 copy-start.7

commit v2 on v1

--- a/solution.py
+++ b/solution.py
@@ -185,12 +185,12 @@
         if late is not None:
             one[0], late[0][-1] = barrier((one[0], late[0][-1]))
             two[0], late[1][-1] = barrier((two[0], late[1][-1]))
-            chunk_0, (w_lo, w_hi) = joined(late[0], (w_lo, w_hi))
+            chunk_0, _ = joined(late[0])
             partial = weight_term(chunk_0)
             chunk_0, partial = barrier((chunk_0, partial))
             upper, lower, *out = sends(partial)
             owned.append(second(upper, lower, *first(*out)))
-            chunk_1, _ = joined(late[1])
+            chunk_1, (w_lo, w_hi) = joined(late[1], (w_lo, w_hi))
             partial = weight_term(chunk_1)
             chunk_1, partial = barrier((chunk_1, partial))
             upper, lower, *out = sends(partial)
@@ -199,11 +199,9 @@
             total = add_term(total, chunk_0, part[pair - 2], weights)
             total = add_term(total, chunk_1, part[pair - 1], weights)
         for step in range(1, chips):
-            if late is not None and step == 2:
+            if late is not None and step == chips - 1:
                 one[-1], owned[-2] = barrier((one[-1], owned[-2]))
-            if late is not None and step == 3:
-                one[-1], owned[-1] = barrier((one[-1], owned[-1]))
-                two[-1], total = barrier((two[-1], total))
+                two[-1], total, owned[-1] = barrier((two[-1], total, owned[-1]))
             if late is None and step == chips - 1:
                 two[-1], w_x, w_y = barrier((two[-1], w_x, w_y))
                 w_lo = partner(w_y[:half_rows], "dp", 1)
@@ -219,7 +217,7 @@
     total = add_term(total, chunk_0, part[-2], weights)
     chunk_1, (total,) = joined(late[1], (total,))
     partial = weight_term(chunk_1)
-    chunk_1, partial, *got = barrier((chunk_1, partial, *got))
+    chunk_1, partial = barrier((chunk_1, partial))
     owned.append(second(upper, lower, *got))
     upper, lower, *out = sends(partial)
     owned.append(second(upper, lower, *first(*out)))

time: 257 us -> 239 us (0.930)
  waiting for transfers between devices: 153 us -> 128 us
  starting transfers between devices: 31.4 us -> 41.2 us
  matrix products: 23.9 us -> 21 us
    ppermute x12, waiting for transfers between devices: 92.9 us -> 45.1 us  [hop(): return lax.ppermute(slot, 'tensor', ring)]
    ppermute x38, waiting for transfers between devices: 59.7 us -> 83.2 us  [partner(): return lax.ppermute(value, axis, pairs)]
    ppermute x12, starting transfers between devices: 7.66 us -> 12.8 us  [hop(): return lax.ppermute(slot, 'tensor', ring)]
    ppermute x38, starting transfers between devices: 23.7 us -> 28.4 us  [partner(): return lax.ppermute(value, axis, pairs)]
    dot_general x4, matrix products: 14.6 us -> 11.7 us  [weight_term(): lax.dot_general(chunk, attended, (((0,), (0,)), ((), ())), preferred_elem...]
    unnamed x58 -> x60, local copies, waits for them, and re-layouts: 16.9 us -> 18.3 us
  transfers between devices with their start and end apart: 50 -> 50, of which waited for: 24 -> 20; matrix products, arithmetic and copies ran while one was open for 21% -> 22% of each run, Pallas kernels for 0% -> 5%
where the time goes in v2:
time: 239 us
  waiting for transfers between devices  128 us (54%)
  starting transfers between devices  41.2 us (17%)
  local copies, waits for them, and re-layouts  30.9 us (13%)
  matrix products  21 us (9%)
  Pallas kernels  11.6 us (5%)
  other arithmetic  4.28 us (2%)
    ppermute x38, waiting for transfers between devices, partner(): return lax.ppermute(value, axis, pairs)  83.2 us
    ppermute x12, waiting for transfers between devices, hop(): return lax.ppermute(slot, 'tensor', ring)  45.1 us
    ppermute x38, starting transfers between devices, partner(): return lax.ppermute(value, axis, pairs)  28.4 us
    unnamed x60, local copies, waits for them, and re-layouts  18.3 us
    ppermute x12, starting transfers between devices, hop(): return lax.ppermute(slot, 'tensor', ring)  12.8 us
    dot_general x4, matrix products, weight_term(): lax.dot_general(chunk, attended, (((0,), (0,)), ((), ())), preferred_elem...  11.7 us
    pallas_call x1, Pallas kernels, attention_grads(): pl.pallas_call(functools.partial(attention_kernel, 256), grid=(heads,), i...  11.6 us
    dot_general x4, matrix products, add_term(): term = jnp.dot(chunk, weight, preferred_element_type=jnp.float32)  9.29 us
  transfers between devices with their start and end apart: 50, of which 20 were waited for; matrix products, arithmetic and copies ran while one was open for 22% of the time, Pallas kernels for 5%

profile of v2, /device:TPU:0, one launch (start us, length us, event | category | flops | bytes accessed | tf_op | source)
XLA Modules:
  0.0 238.8 jit_solution(12612139817514531887)
XLA Ops:
  0.7 2.6 %constant_dynamic-slice_fusion.3 = (bf16[128,512]{1,0:T(8,128)(2,1)S(1)}, bf16[128,512]{1,0:T(8,128)(2,1)S(1)}, bf16[128,512]{1,0:T(8,128)(2,1)S(1)}, bf16[128,5...) fusion(bf16[128,8192]{1,0:T(8,128)(2,1)} %param.7, ...), kind=kLoop, calls=%fused_computation.151 | loop fusion | bytes 4194368 | tf_op jit(solution)/shard_map/dynamic_slice | solution.py:138
  3.9 2.6 %collective-permute-start.8 = (bf16[128,2048]{1,0:T(8,128)(2,1)S(1)}, bf16[128,2048]{1,0:T(8,128)(2,1)}, u32[]{:S(2)}, u32[]{:S(2)}) collective-permute-start(bf16[128,2048]{1,0:T(8,128)(2,1)S(1)} %pad_maximum_fusion.3), channel_id=1, source_target_pairs={{0,2},{1,3},{2,4},{3,5},{4,6},{5,7},{6,0},{7,1},{8,10},{9,11},{10,... | collective-permute-start | bytes 1572872 | tf_op jit(solution)/shard_map/ppermute | solution.py:145
  6.6 1.6 collective-permute-start
  8.2 1.5 collective-permute-start.2
  9.7 0.9 constant_dynamic-update-slice_fusion.7
  12.6 0.9 pad_maximum_fusion.1
  13.5 0.9 pad_maximum_fusion.4
  15.0 2.9 %fusion.68 = (bf16[512,512]{1,0:T(8,128)(2,1)}, bf16[512,512]{1,0:T(8,128)(2,1)}, bf16[512,512]{1,0:T(8,128)(2,1)}, bf16[512,512]{1,0:T(8,128)(2,1)}) fusion(bf16[2048,512]{1,0:T(8,128)(2,1)} %param.8), kind=kLoop, calls=%fused_computation.172 | loop fusion | bytes 4194304 | tf_op jit(solution)/shard_map/slice | solution.py:110
  19.3 2.2 collective-permute-done.8
  22.1 1.1 constant_dynamic-slice_fusion.16
  24.1 2.0 constant_dynamic-update-slice_fusion.6
  26.1 17.5 %collective-permute-done.10 = bf16[128,2048]{1,0:T(8,128)(2,1)} collective-permute-done((bf16[128,2048]{1,0:T(8,128)(2,1)}, bf16[128,2048]{1,0:T(8,128)(2,1)}, u32[]{:S(2)}, u32[]{:S(2)}) %collective-permute-start.10) | collective-permute-done | bytes 524320 | tf_op jit(solution)/shard_map/ppermute | solution.py:145
  43.7 1.9 constant_dynamic-update-slice_fusion.5
  45.5 1.5 collective-permute-start.3
  47.1 1.3 collective-permute-start.1
  48.4 1.9 constant_dynamic-update-slice_fusion.4
  50.2 1.9 constant_dynamic-update-slice_fusion.3
  52.1 8.3 %collective-permute-done.12 = bf16[128,2048]{1,0:T(8,128)(2,1)S(1)} collective-permute-done((bf16[128,2048]{1,0:T(8,128)(2,1)}, bf16[128,2048]{1,0:T(8,128)(2,1)S(1)}, u32[]{:S(2)}, u32[]{:S(2)}) %collective-permute-start.12) | collective-permute-done | bytes 524320 | tf_op jit(solution)/shard_map/ppermute | solution.py:145
  61.8 0.9 constant_dynamic-update-slice_fusion.1
  64.0 4.6 %convolution_convert_fusion.3 = bf16[2048,512]{1,0:T(8,128)(2,1)S(1)} fusion(bf16[1024,2048]{1,0:T(8,128)(2,1)} %constant_dynamic-update-slice_fusion, bf16[1024,512]{1,0:T(8,128)(2,1)S(1)} %copy-done.10), kind=kOutput, calls=%fused_computation.3 | convolution fusion | flops 2148532224 | bytes 7340032 | tf_op jit(solution)/shard_map/dot_general | solution.py:148
  68.6 3.1 %collective-permute-done.1 = bf16[128,2048]{1,0:T(8,128)(2,1)S(1)} collective-permute-done((bf16[128,2048]{1,0:T(8,128)(2,1)}, bf16[128,2048]{1,0:T(8,128)(2,1)S(1)}, u32[]{:S(2)}, u32[]{:S(2)}) %collective-permute-start.1) | collective-permute-done | bytes 524320 | tf_op jit(solution)/shard_map/ppermute | solution.py:145
  71.7 22.1 %collective-permute-done.3 = bf16[2048,512]{1,0:T(8,128)(2,1)S(1)} collective-permute-done((bf16[2048,512]{1,0:T(8,128)(2,1)}, bf16[2048,512]{1,0:T(8,128)(2,1)S(1)}, u32[]{:S(2)}, u32[]{:S(2)}) %collective-permute-start.3) | collective-permute-done | bytes 2097184 | tf_op jit(solution)/shard_map/ppermute | solution.py:18
  93.8 1.0 collective-permute-start.4
  94.9 1.6 collective-permute-start.28
  96.4 1.5 collective-permute-start.30
  97.9 1.8 fusion.69
  100.5 1.3 slice.274
  101.8 7.9 %collective-permute-done.28 = bf16[2,256,512]{2,1,0:T(8,128)(2,1)S(1)} collective-permute-done((bf16[2,256,512]{2,1,0:T(8,128)(2,1)S(1)}, bf16[2,256,512]{2,1,0:T(8,128)(2,1)S(1)}, u32[]{:S(2)}, u32[]{:S(2)}) %collective-permute-start.28) | collective-permute-done | bytes 524320 | tf_op jit(solution)/shard_map/ppermute | solution.py:18
  109.7 1.5 collective-permute-start.15
  112.0 1.5 collective-permute-start.31
  113.5 1.6 collective-permute-start.27
  115.2 22.0 %collective-permute-done.29 = bf16[256,512]{1,0:T(8,128)(2,1)S(1)} collective-permute-done((bf16[256,512]{1,0:T(8,128)(2,1)S(1)}, bf16[256,512]{1,0:T(8,128)(2,1)S(1)}, u32[]{:S(2)}, u32[]{:S(2)}) %collective-permute-start.29) | collective-permute-done | bytes 262176 | tf_op jit(solution)/shard_map/ppermute | solution.py:18
  138.1 1.6 collective-permute-start.5
  140.4 1.1 constant_dynamic-update-slice_fusion.13
  141.5 2.3 collective-permute-start.33
  144.2 2.4 convolution_convert_fusion.2
  146.8 1.2 collective-permute-start.20
  147.9 1.5 collective-permute-start.22
  149.5 2.3 fusion.8
  151.8 2.3 fusion.34
  155.1 10.8 %collective-permute-done.33 = bf16[128,2048]{1,0:T(8,128)(2,1)S(1)} collective-permute-done((bf16[128,2048]{1,0:T(8,128)(2,1)S(1)}, bf16[128,2048]{1,0:T(8,128)(2,1)S(1)}, u32[]{:S(2)}, u32[]{:S(2)}) %collective-permute-start.33) | collective-permute-done | bytes 524320 | tf_op jit(solution)/shard_map/ppermute | solution.py:145
  166.8 1.6 collective-permute-start.21
  168.4 1.1 collective-permute-start.23
  169.6 2.4 convolution_convert_fusion.1
  172.0 2.3 fusion.16
  175.1 1.5 collective-permute-start.44
  176.6 1.1 collective-permute-start.42
  179.2 9.0 %collective-permute-done.44 = bf16[2,256,512]{2,1,0:T(8,128)(2,1)S(1)} collective-permute-done((bf16[2,256,512]{2,1,0:T(8,128)(2,1)S(1)}, bf16[2,256,512]{2,1,0:T(8,128)(2,1)S(1)}, u32[]{:S(2)}, u32[]{:S(2)}) %collective-permute-start.44) | collective-permute-done | bytes 524320 | tf_op jit(solution)/shard_map/ppermute | solution.py:18
  188.1 1.2 collective-permute-done.42
  189.5 1.6 collective-permute-start.43
  191.1 1.1 collective-permute-start.45
  192.2 2.6 %collective-permute-done.38 = bf16[128,2048]{1,0:T(8,128)(2,1)S(1)} collective-permute-done((bf16[128,2048]{1,0:T(8,128)(2,1)S(1)}, bf16[128,2048]{1,0:T(8,128)(2,1)S(1)}, u32[]{:S(2)}, u32[]{:S(2)}) %collective-permute-start.38) | collective-permute-done | bytes 524320 | tf_op jit(solution)/shard_map/ppermute | solution.py:145
  194.9 1.1 collective-permute-done.43
  196.7 2.4 convolution_convert_fusion
  199.1 2.3 add_convert_fusion
  201.8 11.6 %attention_grads.1 = (bf16[1024,512]{1,0:T(8,128)(2,1)}, f32[128,1024]{1,0:T(8,128)S(1)}, f32[128,1024]{1,0:T(8,128)S(1)}) custom-call(bf16[1024,512]{1,0:T(8,128)(2,1)S(1)} %copy-done.1, bf16[1024,128]{1,0:T(8,128)(2,1)S(1)} %get-tuple-element.117.k_ref, bf16[128,1024]{1,0:T(8,128)(2,1)S(1)} %bitcast.101, bf16[1024,128]{1,0:T(8,128)(2,1)S(1)} %get-tuple-element.116.v_ref, ...), custom_call_target="tpu_custom_call" | custom-call | flops 5368709120 | bytes 5242880 | tf_op jit(solution)/shard_map/attention_grads/pallas_call | solution.py:72
  213.7 1.2 collective-permute-start.48
  215.0 1.1 collective-permute-start.46
  216.5 11.6 %collective-permute-done.48 = bf16[2,256,512]{2,1,0:T(8,128)(2,1)S(1)} collective-permute-done((bf16[2,256,512]{2,1,0:T(8,128)(2,1)S(1)}, bf16[2,256,512]{2,1,0:T(8,128)(2,1)S(1)}, u32[]{:S(2)}, u32[]{:S(2)}) %collective-permute-start.48) | collective-permute-done | bytes 524320 | tf_op jit(solution)/shard_map/ppermute | solution.py:18
  228.0 1.0 collective-permute-done.46
  229.2 0.9 collective-permute-start.47
  230.2 1.0 collective-permute-start.49
  231.8 4.9 %collective-permute-done.47 = bf16[256,512]{1,0:T(8,128)(2,1)S(1)} collective-permute-done((bf16[256,512]{1,0:T(8,128)(2,1)S(1)}, bf16[256,512]{1,0:T(8,128)(2,1)S(1)}, u32[]{:S(2)}, u32[]{:S(2)}) %collective-permute-start.47) | collective-permute-done | bytes 262176 | tf_op jit(solution)/shard_map/ppermute | solution.py:18
  237.5 1.3 copy-done.8
  (161 shorter events, 20.0 us)
Async XLA Ops:
  0.6 9.9 %copy-start = (bf16[1024,512]{1,0:T(8,128)(2,1)S(1)}, bf16[1024,512]{1,0:T(8,128)(2,1)}, u32[]{:S(2)}) copy-start(bf16[1024,512]{1,0:T(8,128)(2,1)} %o_ref.1) | copy-start | bytes 3145732
  3.3 20.8 %collective-permute-start.7 = (bf16[128,2048]{1,0:T(8,128)(2,1)S(1)}, bf16[128,2048]{1,0:T(8,128)(2,1)}, u32[]{:S(2)}, u32[]{:S(2)}) collective-permute-start(bf16[128,2048]{1,0:T(8,128)(2,1)S(1)} %pad_maximum_fusion.3), channel_id=1, source_target_pairs={{0,1},{1,0},{2,3},{3,2},{4,5},{5,4},{6,7},{7,6},{8,9},{9,8},{10,11... | collective-permute-start | bytes 1572872 | tf_op jit(solution)/shard_map/ppermute | solution.py:18
  3.9 17.5 %collective-permute-start.8 = (bf16[128,2048]{1,0:T(8,128)(2,1)S(1)}, bf16[128,2048]{1,0:T(8,128)(2,1)}, u32[]{:S(2)}, u32[]{:S(2)}) collective-permute-start(bf16[128,2048]{1,0:T(8,128)(2,1)S(1)} %pad_maximum_fusion.3), channel_id=1, source_target_pairs={{0,2},{1,3},{2,4},{3,5},{4,6},{5,7},{6,0},{7,1},{8,10},{9,11},{10,... | collective-permute-start | bytes 1572872 | tf_op jit(solution)/shard_map/ppermute | solution.py:145
  6.6 39.0 %collective-permute-start = (bf16[128,2048]{1,0:T(8,128)(2,1)S(1)}, bf16[128,2048]{1,0:T(8,128)(2,1)}, u32[]{:S(2)}, u32[]{:S(2)}) collective-permute-start(bf16[128,2048]{1,0:T(8,128)(2,1)S(1)} %pad_maximum_fusion.2), channel_id=1, source_target_pairs={{0,2},{1,3},{2,4},{3,5},{4,6},{5,7},{6,0},{7,1},{8,10},{9,11},{10,... | collective-permute-start | bytes 1572872 | tf_op jit(solution)/shard_map/ppermute | solution.py:145
  8.2 63.5 %collective-permute-start.2 = (bf16[2048,512]{1,0:T(8,128)(2,1)}, bf16[2048,512]{1,0:T(8,128)(2,1)}, u32[]{:S(2)}, u32[]{:S(2)}) collective-permute-start(bf16[2048,512]{1,0:T(8,128)(2,1)} %param.8), channel_id=1, source_target_pairs={{0,8},{8,0},{16,24},{24,16},{1,9},{9,1},{17,25},{25,17},{2,10},{10... | collective-permute-start | bytes 6291464 | tf_op jit(solution)/shard_map/ppermute | solution.py:18
  21.4 22.2 %collective-permute-start.10 = (bf16[128,2048]{1,0:T(8,128)(2,1)}, bf16[128,2048]{1,0:T(8,128)(2,1)}, u32[]{:S(2)}, u32[]{:S(2)}) collective-permute-start(bf16[128,2048]{1,0:T(8,128)(2,1)} %collective-permute-done.8), channel_id=1, source_target_pairs={{0,2},{1,3},{2,4},{3,5},{4,6},{5,7},{6,0},{7,1},{8,10},{9,11},{10,... | collective-permute-start | bytes 1572872 | tf_op jit(solution)/shard_map/ppermute | solution.py:145
  23.2 23.9 %collective-permute-start.9 = (bf16[128,2048]{1,0:T(8,128)(2,1)}, bf16[128,2048]{1,0:T(8,128)(2,1)}, u32[]{:S(2)}, u32[]{:S(2)}) collective-permute-start(bf16[128,2048]{1,0:T(8,128)(2,1)} %collective-permute-done.8), channel_id=1, source_target_pairs={{0,1},{1,0},{2,3},{3,2},{4,5},{5,4},{6,7},{7,6},{8,9},{9,8},{10,11... | collective-permute-start | bytes 1572872 | tf_op jit(solution)/shard_map/ppermute | solution.py:18
  24.1 36.4 %copy-start.3 = (bf16[128,2048]{1,0:T(8,128)(2,1)S(1)}, bf16[128,2048]{1,0:T(8,128)(2,1)}, u32[]{:S(2)}) copy-start(bf16[128,2048]{1,0:T(8,128)(2,1)} %pad_maximum_fusion.4) | copy-start | bytes 1572868
  24.1 39.9 %copy-start.10 = (bf16[1024,512]{1,0:T(8,128)(2,1)S(1)}, bf16[1024,512]{1,0:T(8,128)(2,1)}, u32[]{:S(2)}) copy-start(bf16[1024,512]{1,0:T(8,128)(2,1)} %dynamic-slice_dynamic-update-slice_fusion) | copy-start | bytes 3145732
  43.6 16.8 %collective-permute-start.11 = (bf16[128,2048]{1,0:T(8,128)(2,1)}, bf16[128,2048]{1,0:T(8,128)(2,1)S(1)}, u32[]{:S(2)}, u32[]{:S(2)}) collective-permute-start(bf16[128,2048]{1,0:T(8,128)(2,1)} %collective-permute-done.10), channel_id=1, source_target_pairs={{0,1},{1,0},{2,3},{3,2},{4,5},{5,4},{6,7},{7,6},{8,9},{9,8},{10,11... | collective-permute-start | bytes 1572872 | tf_op jit(solution)/shard_map/ppermute | solution.py:18
  43.6 16.8 %collective-permute-start.12 = (bf16[128,2048]{1,0:T(8,128)(2,1)}, bf16[128,2048]{1,0:T(8,128)(2,1)S(1)}, u32[]{:S(2)}, u32[]{:S(2)}) collective-permute-start(bf16[128,2048]{1,0:T(8,128)(2,1)} %collective-permute-done.10), channel_id=1, source_target_pairs={{0,2},{1,3},{2,4},{3,5},{4,6},{5,7},{6,0},{7,1},{8,10},{9,11},{10,... | collective-permute-start | bytes 1572872 | tf_op jit(solution)/shard_map/ppermute | solution.py:145
  45.5 48.3 %collective-permute-start.3 = (bf16[2048,512]{1,0:T(8,128)(2,1)}, bf16[2048,512]{1,0:T(8,128)(2,1)S(1)}, u32[]{:S(2)}, u32[]{:S(2)}) collective-permute-start(bf16[2048,512]{1,0:T(8,128)(2,1)} %param.8), channel_id=1, source_target_pairs={{0,16},{8,24},{16,0},{24,8},{1,17},{9,25},{17,1},{25,9},{2,18},{10... | collective-permute-start | bytes 6291464 | tf_op jit(solution)/shard_map/ppermute | solution.py:18
  47.1 24.6 %collective-permute-start.1 = (bf16[128,2048]{1,0:T(8,128)(2,1)}, bf16[128,2048]{1,0:T(8,128)(2,1)S(1)}, u32[]{:S(2)}, u32[]{:S(2)}) collective-permute-start(bf16[128,2048]{1,0:T(8,128)(2,1)} %collective-permute-done), channel_id=1, source_target_pairs={{0,2},{1,3},{2,4},{3,5},{4,6},{5,7},{6,0},{7,1},{8,10},{9,11},{10,... | collective-permute-start | bytes 1572872 | tf_op jit(solution)/shard_map/ppermute | solution.py:145
  60.5 39.4 %collective-permute-start.24 = (bf16[128,2048]{1,0:T(8,128)(2,1)S(1)}, bf16[128,2048]{1,0:T(8,128)(2,1)S(1)}, u32[]{:S(2)}, u32[]{:S(2)}) collective-permute-start(bf16[128,2048]{1,0:T(8,128)(2,1)S(1)} %copy-done.3), channel_id=1, source_target_pairs={{0,1},{1,0},{2,3},{3,2},{4,5},{5,4},{6,7},{7,6},{8,9},{9,8},{10,11... | collective-permute-start | bytes 1572872 | tf_op jit(solution)/shard_map/ppermute | solution.py:18
  60.5 2.7 %collective-permute-start.13 = (bf16[128,2048]{1,0:T(8,128)(2,1)S(1)}, bf16[128,2048]{1,0:T(8,128)(2,1)S(1)}, u32[]{:S(2)}, u32[]{:S(2)}) collective-permute-start(bf16[128,2048]{1,0:T(8,128)(2,1)S(1)} %collective-permute-done.12), channel_id=1, source_target_pairs={{0,1},{1,0},{2,3},{3,2},{4,5},{5,4},{6,7},{7,6},{8,9},{9,8},{10,11... | collective-permute-start | bytes 1572872 | tf_op jit(solution)/shard_map/ppermute | solution.py:18
  63.1 37.3 %collective-permute-start.25 = (bf16[128,2048]{1,0:T(8,128)(2,1)S(1)}, bf16[128,2048]{1,0:T(8,128)(2,1)S(1)}, u32[]{:S(2)}, u32[]{:S(2)}) collective-permute-start(bf16[128,2048]{1,0:T(8,128)(2,1)S(1)} %copy-done.3), channel_id=1, source_target_pairs={{0,2},{1,3},{2,4},{3,5},{4,6},{5,7},{6,0},{7,1},{8,10},{9,11},{10,... | collective-permute-start | bytes 1572872 | tf_op jit(solution)/shard_map/ppermute | solution.py:145
  93.8 18.2 %collective-permute-start.4 = (bf16[128,2048]{1,0:T(8,128)(2,1)S(1)}, bf16[128,2048]{1,0:T(8,128)(2,1)S(1)}, u32[]{:S(2)}, u32[]{:S(2)}) collective-permute-start(bf16[128,2048]{1,0:T(8,128)(2,1)S(1)} %collective-permute-done.1), channel_id=1, source_target_pairs={{0,2},{1,3},{2,4},{3,5},{4,6},{5,7},{6,0},{7,1},{8,10},{9,11},{10,... | collective-permute-start | bytes 1572872 | tf_op jit(solution)/shard_map/ppermute | solution.py:145
  94.9 14.9 %collective-permute-start.28 = (bf16[2,256,512]{2,1,0:T(8,128)(2,1)S(1)}, bf16[2,256,512]{2,1,0:T(8,128)(2,1)S(1)}, u32[]{:S(2)}, u32[]{:S(2)}) collective-permute-start(bf16[2,256,512]{2,1,0:T(8,128)(2,1)S(1)} %pad_maximum_fusion.7), channel_id=1, source_target_pairs={{0,8},{8,0},{16,24},{24,16},{1,9},{9,1},{17,25},{25,17},{2,10},{10... | collective-permute-start | bytes 1572872 | tf_op jit(solution)/shard_map/ppermute | solution.py:18
  96.4 14.8 %collective-permute-start.30 = (bf16[2,256,512]{2,1,0:T(8,128)(2,1)S(1)}, bf16[2,256,512]{2,1,0:T(8,128)(2,1)S(1)}, u32[]{:S(2)}, u32[]{:S(2)}) collective-permute-start(bf16[2,256,512]{2,1,0:T(8,128)(2,1)S(1)} %slice.364), channel_id=1, source_target_pairs={{0,16},{8,24},{16,0},{24,8},{1,17},{9,25},{17,1},{25,9},{2,18},{10... | collective-permute-start | bytes 1572872 | tf_op jit(solution)/shard_map/ppermute | solution.py:18
  99.8 38.3 %collective-permute-start.14 = (bf16[1024,512]{1,0:T(8,128)(2,1)S(1)}, bf16[1024,512]{1,0:T(8,128)(2,1)S(1)}, u32[]{:S(2)}, u32[]{:S(2)}) collective-permute-start(bf16[1024,512]{1,0:T(8,128)(2,1)S(1)} %slice.273), channel_id=1, source_target_pairs={{0,8},{8,0},{16,24},{24,16},{1,9},{9,1},{17,25},{25,17},{2,10},{10... | collective-permute-start | bytes 3145736 | tf_op jit(solution)/shard_map/ppermute | solution.py:18
  100.4 13.1 %collective-permute-start.26 = (bf16[128,2048]{1,0:T(8,128)(2,1)S(1)}, bf16[128,2048]{1,0:T(8,128)(2,1)S(1)}, u32[]{:S(2)}, u32[]{:S(2)}) collective-permute-start(bf16[128,2048]{1,0:T(8,128)(2,1)S(1)} %collective-permute-done.25), channel_id=1, source_target_pairs={{0,1},{1,0},{2,3},{3,2},{4,5},{5,4},{6,7},{7,6},{8,9},{9,8},{10,11... | collective-permute-start | bytes 1572872 | tf_op jit(solution)/shard_map/ppermute | solution.py:18
  109.7 30.0 %collective-permute-start.15 = (bf16[1024,512]{1,0:T(8,128)(2,1)S(1)}, bf16[1024,512]{1,0:T(8,128)(2,1)S(1)}, u32[]{:S(2)}, u32[]{:S(2)}) collective-permute-start(bf16[1024,512]{1,0:T(8,128)(2,1)S(1)} %slice.274), channel_id=1, source_target_pairs={{0,16},{8,24},{16,0},{24,8},{1,17},{9,25},{17,1},{25,9},{2,18},{10... | collective-permute-start | bytes 3145736 | tf_op jit(solution)/shard_map/ppermute | solution.py:18
  111.4 25.8 %collective-permute-start.29 = (bf16[256,512]{1,0:T(8,128)(2,1)S(1)}, bf16[256,512]{1,0:T(8,128)(2,1)S(1)}, u32[]{:S(2)}, u32[]{:S(2)}) collective-permute-start(bf16[256,512]{1,0:T(8,128)(2,1)S(1)} %get-tuple-element.82), channel_id=1, source_target_pairs={{0,16},{8,24},{16,0},{24,8},{1,17},{9,25},{17,1},{25,9},{2,18},{10... | collective-permute-start | bytes 786440 | tf_op jit(solution)/shard_map/ppermute | solution.py:18
  112.0 25.2 %collective-permute-start.31 = (bf16[256,512]{1,0:T(8,128)(2,1)S(1)}, bf16[256,512]{1,0:T(8,128)(2,1)S(1)}, u32[]{:S(2)}, u32[]{:S(2)}) collective-permute-start(bf16[256,512]{1,0:T(8,128)(2,1)S(1)} %get-tuple-element.83), channel_id=1, source_target_pairs={{0,8},{8,0},{16,24},{24,16},{1,9},{9,1},{17,25},{25,17},{2,10},{10... | collective-permute-start | bytes 786440 | tf_op jit(solution)/shard_map/ppermute | solution.py:18
  113.5 24.4 %collective-permute-start.27 = (bf16[128,2048]{1,0:T(8,128)(2,1)S(1)}, bf16[128,2048]{1,0:T(8,128)(2,1)S(1)}, u32[]{:S(2)}, u32[]{:S(2)}) collective-permute-start(bf16[128,2048]{1,0:T(8,128)(2,1)S(1)} %collective-permute-done.25), channel_id=1, source_target_pairs={{0,2},{1,3},{2,4},{3,5},{4,6},{5,7},{6,0},{7,1},{8,10},{9,11},{10,... | collective-permute-start | bytes 1572872 | tf_op jit(solution)/shard_map/ppermute | solution.py:145
  137.1 2.8 %collective-permute-start.16 = (bf16[128,2048]{1,0:T(8,128)(2,1)S(1)}, bf16[128,2048]{1,0:T(8,128)(2,1)S(1)}, u32[]{:S(2)}, u32[]{:S(2)}) collective-permute-start(bf16[128,2048]{1,0:T(8,128)(2,1)S(1)} %pad_maximum_fusion.2), channel_id=1, source_target_pairs={{0,1},{1,0},{2,3},{3,2},{4,5},{5,4},{6,7},{7,6},{8,9},{9,8},{10,11... | collective-permute-start | bytes 1572872 | tf_op jit(solution)/shard_map/ppermute | solution.py:18
  137.2 4.3 %collective-permute-start.17 = (bf16[128,2048]{1,0:T(8,128)(2,1)}, bf16[128,2048]{1,0:T(8,128)(2,1)S(1)}, u32[]{:S(2)}, u32[]{:S(2)}) collective-permute-start(bf16[128,2048]{1,0:T(8,128)(2,1)} %collective-permute-done), channel_id=1, source_target_pairs={{0,1},{1,0},{2,3},{3,2},{4,5},{5,4},{6,7},{7,6},{8,9},{9,8},{10,11... | collective-permute-start | bytes 1572872 | tf_op jit(solution)/shard_map/ppermute | solution.py:18
  137.9 6.0 %collective-permute-start.18 = (bf16[128,2048]{1,0:T(8,128)(2,1)S(1)}, bf16[128,2048]{1,0:T(8,128)(2,1)S(1)}, u32[]{:S(2)}, u32[]{:S(2)}) collective-permute-start(bf16[128,2048]{1,0:T(8,128)(2,1)S(1)} %collective-permute-done.1), channel_id=1, source_target_pairs={{0,1},{1,0},{2,3},{3,2},{4,5},{5,4},{6,7},{7,6},{8,9},{9,8},{10,11... | collective-permute-start | bytes 1572872 | tf_op jit(solution)/shard_map/ppermute | solution.py:18
  138.1 16.6 %collective-permute-start.5 = (bf16[128,2048]{1,0:T(8,128)(2,1)S(1)}, bf16[128,2048]{1,0:T(8,128)(2,1)S(1)}, u32[]{:S(2)}, u32[]{:S(2)}) collective-permute-start(bf16[128,2048]{1,0:T(8,128)(2,1)S(1)} %pad_maximum_fusion.1), channel_id=1, source_target_pairs={{0,2},{1,3},{2,4},{3,5},{4,6},{5,7},{6,0},{7,1},{8,10},{9,11},{10,... | collective-permute-start | bytes 1572872 | tf_op jit(solution)/shard_map/ppermute | solution.py:145
  139.7 4.4 %collective-permute-start.19 = (bf16[128,2048]{1,0:T(8,128)(2,1)S(1)}, bf16[128,2048]{1,0:T(8,128)(2,1)S(1)}, u32[]{:S(2)}, u32[]{:S(2)}) collective-permute-start(bf16[128,2048]{1,0:T(8,128)(2,1)S(1)} %collective-permute-done.4), channel_id=1, source_target_pairs={{0,1},{1,0},{2,3},{3,2},{4,5},{5,4},{6,7},{7,6},{8,9},{9,8},{10,11... | collective-permute-start | bytes 1572872 | tf_op jit(solution)/shard_map/ppermute | solution.py:18
  140.0 14.8 %collective-permute-start.32 = (bf16[128,2048]{1,0:T(8,128)(2,1)S(1)}, bf16[128,2048]{1,0:T(8,128)(2,1)S(1)}, u32[]{:S(2)}, u32[]{:S(2)}) collective-permute-start(bf16[128,2048]{1,0:T(8,128)(2,1)S(1)} %collective-permute-done.27), channel_id=1, source_target_pairs={{0,1},{1,0},{2,3},{3,2},{4,5},{5,4},{6,7},{7,6},{8,9},{9,8},{10,11... | collective-permute-start | bytes 1572872 | tf_op jit(solution)/shard_map/ppermute | solution.py:18
  141.5 24.5 %collective-permute-start.33 = (bf16[128,2048]{1,0:T(8,128)(2,1)S(1)}, bf16[128,2048]{1,0:T(8,128)(2,1)S(1)}, u32[]{:S(2)}, u32[]{:S(2)}) collective-permute-start(bf16[128,2048]{1,0:T(8,128)(2,1)S(1)} %collective-permute-done.27), channel_id=1, source_target_pairs={{0,2},{1,3},{2,4},{3,5},{4,6},{5,7},{6,0},{7,1},{8,10},{9,11},{10,... | collective-permute-start | bytes 1572872 | tf_op jit(solution)/shard_map/ppermute | solution.py:145
  144.2 5.2 %copy-start.7 = (bf16[512,512]{1,0:T(8,128)(2,1)S(1)}, bf16[512,512]{1,0:T(8,128)(2,1)}, u32[]{:S(2)}) copy-start(bf16[512,512]{1,0:T(8,128)(2,1)} %get-tuple-element.69) | copy-start | bytes 1572868
  146.8 19.3 %collective-permute-start.20 = (bf16[2,256,512]{2,1,0:T(8,128)(2,1)S(1)}, bf16[2,256,512]{2,1,0:T(8,128)(2,1)S(1)}, u32[]{:S(2)}, u32[]{:S(2)}) collective-permute-start(bf16[2,256,512]{2,1,0:T(8,128)(2,1)S(1)} %pad_maximum_fusion.5), channel_id=1, source_target_pairs={{0,8},{8,0},{16,24},{24,16},{1,9},{9,1},{17,25},{25,17},{2,10},{10... | collective-permute-start | bytes 1572872 | tf_op jit(solution)/shard_map/ppermute | solution.py:18
  147.9 18.7 %collective-permute-start.22 = (bf16[2,256,512]{2,1,0:T(8,128)(2,1)S(1)}, bf16[2,256,512]{2,1,0:T(8,128)(2,1)S(1)}, u32[]{:S(2)}, u32[]{:S(2)}) collective-permute-start(bf16[2,256,512]{2,1,0:T(8,128)(2,1)S(1)} %slice.353), channel_id=1, source_target_pairs={{0,16},{8,24},{16,0},{24,8},{1,17},{9,25},{17,1},{25,9},{2,18},{10... | collective-permute-start | bytes 1572872 | tf_op jit(solution)/shard_map/ppermute | solution.py:18
  149.5 2.3 copy-start.6
  149.5 2.4 copy-start.9
  154.7 23.9 %collective-permute-start.35 = (bf16[128,2048]{1,0:T(8,128)(2,1)S(1)}, bf16[128,2048]{1,0:T(8,128)(2,1)S(1)}, u32[]{:S(2)}, u32[]{:S(2)}) collective-permute-start(bf16[128,2048]{1,0:T(8,128)(2,1)S(1)} %pad_maximum_fusion.1), channel_id=1, source_target_pairs={{0,1},{1,0},{2,3},{3,2},{4,5},{5,4},{6,7},{7,6},{8,9},{9,8},{10,11... | collective-permute-start | bytes 1572872 | tf_op jit(solution)/shard_map/ppermute | solution.py:18
  154.8 23.2 %collective-permute-start.6 = (bf16[128,2048]{1,0:T(8,128)(2,1)S(1)}, bf16[128,2048]{1,0:T(8,128)(2,1)S(1)}, u32[]{:S(2)}, u32[]{:S(2)}) collective-permute-start(bf16[128,2048]{1,0:T(8,128)(2,1)S(1)} %collective-permute-done.5), channel_id=1, source_target_pairs={{0,2},{1,3},{2,4},{3,5},{4,6},{5,7},{6,0},{7,1},{8,10},{9,11},{10,... | collective-permute-start | bytes 1572872 | tf_op jit(solution)/shard_map/ppermute | solution.py:145
  166.0 2.4 %collective-permute-start.34 = (bf16[128,2048]{1,0:T(8,128)(2,1)S(1)}, bf16[128,2048]{1,0:T(8,128)(2,1)S(1)}, u32[]{:S(2)}, u32[]{:S(2)}) collective-permute-start(bf16[128,2048]{1,0:T(8,128)(2,1)S(1)} %collective-permute-done.33), channel_id=1, source_target_pairs={{0,1},{1,0},{2,3},{3,2},{4,5},{5,4},{6,7},{7,6},{8,9},{9,8},{10,11... | collective-permute-start | bytes 1572872 | tf_op jit(solution)/shard_map/ppermute | solution.py:18
  166.1 12.9 %collective-permute-start.36 = (bf16[128,2048]{1,0:T(8,128)(2,1)S(1)}, bf16[128,2048]{1,0:T(8,128)(2,1)S(1)}, u32[]{:S(2)}, u32[]{:S(2)}) collective-permute-start(bf16[128,2048]{1,0:T(8,128)(2,1)S(1)} %collective-permute-done.5), channel_id=1, source_target_pairs={{0,1},{1,0},{2,3},{3,2},{4,5},{5,4},{6,7},{7,6},{8,9},{9,8},{10,11... | collective-permute-start | bytes 1572872 | tf_op jit(solution)/shard_map/ppermute | solution.py:18
  166.8 8.3 %collective-permute-start.21 = (bf16[256,512]{1,0:T(8,128)(2,1)S(1)}, bf16[256,512]{1,0:T(8,128)(2,1)S(1)}, u32[]{:S(2)}, u32[]{:S(2)}) collective-permute-start(bf16[256,512]{1,0:T(8,128)(2,1)S(1)} %get-tuple-element.88), channel_id=1, source_target_pairs={{0,16},{8,24},{16,0},{24,8},{1,17},{9,25},{17,1},{25,9},{2,18},{10... | collective-permute-start | bytes 786440 | tf_op jit(solution)/shard_map/ppermute | solution.py:18
  168.4 8.2 %collective-permute-start.23 = (bf16[256,512]{1,0:T(8,128)(2,1)S(1)}, bf16[256,512]{1,0:T(8,128)(2,1)S(1)}, u32[]{:S(2)}, u32[]{:S(2)}) collective-permute-start(bf16[256,512]{1,0:T(8,128)(2,1)S(1)} %get-tuple-element.89), channel_id=1, source_target_pairs={{0,8},{8,0},{16,24},{24,16},{1,9},{9,1},{17,25},{25,17},{2,10},{10... | collective-permute-start | bytes 786440 | tf_op jit(solution)/shard_map/ppermute | solution.py:18
  169.6 2.4 %copy-start.5 = (bf16[512,512]{1,0:T(8,128)(2,1)S(1)}, bf16[512,512]{1,0:T(8,128)(2,1)}, u32[]{:S(2)}) copy-start(bf16[512,512]{1,0:T(8,128)(2,1)} %get-tuple-element.71) | copy-start | bytes 1572868
  175.1 13.0 %collective-permute-start.44 = (bf16[2,256,512]{2,1,0:T(8,128)(2,1)S(1)}, bf16[2,256,512]{2,1,0:T(8,128)(2,1)S(1)}, u32[]{:S(2)}, u32[]{:S(2)}) collective-permute-start(bf16[2,256,512]{2,1,0:T(8,128)(2,1)S(1)} %slice.389), channel_id=1, source_target_pairs={{0,16},{8,24},{16,0},{24,8},{1,17},{9,25},{17,1},{25,9},{2,18},{10... | collective-permute-start | bytes 1572872 | tf_op jit(solution)/shard_map/ppermute | solution.py:18
  176.6 12.7 %collective-permute-start.42 = (bf16[2,256,512]{2,1,0:T(8,128)(2,1)S(1)}, bf16[2,256,512]{2,1,0:T(8,128)(2,1)S(1)}, u32[]{:S(2)}, u32[]{:S(2)}) collective-permute-start(bf16[2,256,512]{2,1,0:T(8,128)(2,1)S(1)} %pad_maximum_fusion.9), channel_id=1, source_target_pairs={{0,8},{8,0},{16,24},{24,16},{1,9},{9,1},{17,25},{25,17},{2,10},{10... | collective-permute-start | bytes 1572872 | tf_op jit(solution)/shard_map/ppermute | solution.py:18
  178.5 16.2 %collective-permute-start.37 = (bf16[128,2048]{1,0:T(8,128)(2,1)S(1)}, bf16[128,2048]{1,0:T(8,128)(2,1)S(1)}, u32[]{:S(2)}, u32[]{:S(2)}) collective-permute-start(bf16[128,2048]{1,0:T(8,128)(2,1)S(1)} %collective-permute-done.6), channel_id=1, source_target_pairs={{0,1},{1,0},{2,3},{3,2},{4,5},{5,4},{6,7},{7,6},{8,9},{9,8},{10,11... | collective-permute-start | bytes 1572872 | tf_op jit(solution)/shard_map/ppermute | solution.py:18
  178.6 16.1 %collective-permute-start.38 = (bf16[128,2048]{1,0:T(8,128)(2,1)S(1)}, bf16[128,2048]{1,0:T(8,128)(2,1)S(1)}, u32[]{:S(2)}, u32[]{:S(2)}) collective-permute-start(bf16[128,2048]{1,0:T(8,128)(2,1)S(1)} %collective-permute-done.6), channel_id=1, source_target_pairs={{0,2},{1,3},{2,4},{3,5},{4,6},{5,7},{6,0},{7,1},{8,10},{9,11},{10,... | collective-permute-start | bytes 1572872 | tf_op jit(solution)/shard_map/ppermute | solution.py:145
  189.5 6.5 %collective-permute-start.43 = (bf16[256,512]{1,0:T(8,128)(2,1)S(1)}, bf16[256,512]{1,0:T(8,128)(2,1)S(1)}, u32[]{:S(2)}, u32[]{:S(2)}) collective-permute-start(bf16[256,512]{1,0:T(8,128)(2,1)S(1)} %get-tuple-element.65), channel_id=1, source_target_pairs={{0,16},{8,24},{16,0},{24,8},{1,17},{9,25},{17,1},{25,9},{2,18},{10... | collective-permute-start | bytes 786440 | tf_op jit(solution)/shard_map/ppermute | solution.py:18
  191.1 25.1 %collective-permute-start.45 = (bf16[256,512]{1,0:T(8,128)(2,1)S(1)}, bf16[256,512]{1,0:T(8,128)(2,1)S(1)}, u32[]{:S(2)}, u32[]{:S(2)}) collective-permute-start(bf16[256,512]{1,0:T(8,128)(2,1)S(1)} %get-tuple-element.64), channel_id=1, source_target_pairs={{0,8},{8,0},{16,24},{24,16},{1,9},{9,1},{17,25},{25,17},{2,10},{10... | collective-permute-start | bytes 786440 | tf_op jit(solution)/shard_map/ppermute | solution.py:18
  194.8 1.9 collective-permute-start.39
  196.7 2.4 %copy-start.4 = (bf16[512,512]{1,0:T(8,128)(2,1)S(1)}, bf16[512,512]{1,0:T(8,128)(2,1)}, u32[]{:S(2)}) copy-start(bf16[512,512]{1,0:T(8,128)(2,1)} %get-tuple-element.68) | copy-start | bytes 1572868
  199.1 2.6 %copy-start.1 = (bf16[1024,512]{1,0:T(8,128)(2,1)S(1)}, bf16[1024,512]{1,0:T(8,128)(2,1)}, u32[]{:S(2)}) copy-start(bf16[1024,512]{1,0:T(8,128)(2,1)} %q_ref.1) | copy-start | bytes 3145732
  199.1 2.6 %copy-start.2 = (f32[4,1024]{1,0:T(4,128)S(1)}, f32[4,1024]{1,0:T(4,128)}, u32[]{:S(2)}) copy-start(f32[4,1024]{1,0:T(4,128)} %s_ref.1) | copy-start | bytes 49156
  213.5 2.7 %collective-permute-start.40 = (bf16[2,2,32,1024]{3,2,0,1:T(8,128)(2,1)S(1)}, bf16[2,2,32,1024]{3,2,0,1:T(8,128)(2,1)S(1)}, u32[]{:S(2)}, u32[]{:S(2)}) collective-permute-start(bf16[2,2,32,1024]{3,2,0,1:T(8,128)(2,1)S(1)} %fusion.51), channel_id=1, source_target_pairs={{0,1},{1,0},{2,3},{3,2},{4,5},{5,4},{6,7},{7,6},{8,9},{9,8},{10,11... | collective-permute-start | bytes 786440 | tf_op jit(solution)/shard_map/ppermute | solution.py:18
  213.7 14.3 %collective-permute-start.48 = (bf16[2,256,512]{2,1,0:T(8,128)(2,1)S(1)}, bf16[2,256,512]{2,1,0:T(8,128)(2,1)S(1)}, u32[]{:S(2)}, u32[]{:S(2)}) collective-permute-start(bf16[2,256,512]{2,1,0:T(8,128)(2,1)S(1)} %slice.400), channel_id=1, source_target_pairs={{0,16},{8,24},{16,0},{24,8},{1,17},{9,25},{17,1},{25,9},{2,18},{10... | collective-permute-start | bytes 1572872 | tf_op jit(solution)/shard_map/ppermute | solution.py:18
  215.0 14.0 %collective-permute-start.46 = (bf16[2,256,512]{2,1,0:T(8,128)(2,1)S(1)}, bf16[2,256,512]{2,1,0:T(8,128)(2,1)S(1)}, u32[]{:S(2)}, u32[]{:S(2)}) collective-permute-start(bf16[2,256,512]{2,1,0:T(8,128)(2,1)S(1)} %pad_maximum_fusion.10), channel_id=1, source_target_pairs={{0,8},{8,0},{16,24},{24,16},{1,9},{9,1},{17,25},{25,17},{2,10},{10... | collective-permute-start | bytes 1572872 | tf_op jit(solution)/shard_map/ppermute | solution.py:18
  216.4 13.8 %collective-permute-start.41 = (bf16[2,1,32,1024]{3,2,1,0:T(8,128)(2,1)S(1)}, bf16[2,1,32,1024]{3,2,1,0:T(8,128)(2,1)S(1)}, u32[]{:S(2)}, u32[]{:S(2)}) collective-permute-start(bf16[2,1,32,1024]{3,2,1,0:T(8,128)(2,1)S(1)} %fusion.61), channel_id=1, source_target_pairs={{0,2},{1,3},{2,0},{3,1},{4,6},{5,7},{6,4},{7,5},{8,10},{9,11},{10,... | collective-permute-start | bytes 393224 | tf_op jit(solution)/shard_map/ppermute | solution.py:18
  229.2 7.6 %collective-permute-start.47 = (bf16[256,512]{1,0:T(8,128)(2,1)S(1)}, bf16[256,512]{1,0:T(8,128)(2,1)S(1)}, u32[]{:S(2)}, u32[]{:S(2)}) collective-permute-start(bf16[256,512]{1,0:T(8,128)(2,1)S(1)} %get-tuple-element.61), channel_id=1, source_target_pairs={{0,16},{8,24},{16,0},{24,8},{1,17},{9,25},{17,1},{25,9},{2,18},{10... | collective-permute-start | bytes 786440 | tf_op jit(solution)/shard_map/ppermute | solution.py:18
  230.2 7.2 %collective-permute-start.49 = (bf16[256,512]{1,0:T(8,128)(2,1)S(1)}, bf16[256,512]{1,0:T(8,128)(2,1)S(1)}, u32[]{:S(2)}, u32[]{:S(2)}) collective-permute-start(bf16[256,512]{1,0:T(8,128)(2,1)S(1)} %get-tuple-element.60), channel_id=1, source_target_pairs={{0,8},{8,0},{16,24},{24,16},{1,9},{9,1},{17,25},{25,17},{2,10},{10... | collective-permute-start | bytes 786440 | tf_op jit(solution)/shard_map/ppermute | solution.py:18
  237.5 1.3 copy-start.8
